TPU v7x, 256 devices: a whole 4x4x8 slice. The times are simulated.
256 devices in a mesh: expert: 8 (over y, core), shard: 32 (over z, x).
Axes of the slice: x: 4, y: 4, z: 8, core: 2. Of those that a mesh axis runs over, the one named last changes fastest.
Arguments:
- master_down: float32 [16, 6400, 4096], P('expert', None, 'shard'), may hold values from -0.15625 to 0.15625
- second_down: bfloat16 [16, 6400, 4096], P('expert', None, 'shard'), may hold values from -0.0390625 to 0.0390625
- router_weight: float32 [4096, 16], P('shard', 'expert'), may hold values from -0.09375 to 0.09375
- router_gain: float32 [4096], P('shard'), may hold values from 0.25 to 1.75
Outputs:
- final_down: bfloat16 [16, 6400, 4096], P('expert', 'shard')
- scale_down: float32 [16, 6400], P('expert', 'shard')
- serve_router: bfloat16 [4096, 16], replicated
All inputs are finite; a program needn't handle non-finite values.
Results may differ from a plain program's by a relative error of at most 0.0085.
Values may be sent and summed in bfloat16 or wider, within the bound.
No kernel may reach another device: no remote copies, remote signals or barrier semaphores. Data moves between devices by JAX's collectives and lax.ppermute only.
A program may use at most 64 MiB of HBM per device.

v0:
```python
import jax
import jax.numpy as jnp
from jax import lax
from jax.experimental import pallas as pl
from jax.experimental.pallas import tpu as pltpu
from jax.sharding import PartitionSpec as P


RING, CROSS = 8, 4
FIRST_ROWS = 128
PACK_GROUPS = (16, 8, 4, 4)
TILE = 8
NORM_ROWS = 32
VMEM_LIMIT = 32 << 20
ALONG = (4, 3, 5, 2, 6, 1, 7)


def merged(master, second):
    return (master + second.astype(jnp.float32)).astype(jnp.bfloat16)


def packed_kernel(
    master_ref, second_ref, router_ref, gain_ref, out_ref,
    master_vmem, second_vmem, router_vmem, gain_vmem, out_vmem, master_sem, second_sem, out_sem, small_sem,
):
    experts, _, rows, lanes = master_vmem.shape
    steps = len(PACK_GROUPS)

    def at(step):
        return pl.ds(sum(PACK_GROUPS[:step]), PACK_GROUPS[step])

    def copies(step):
        taken = (slice(None), at(step), pl.ds(0, rows))
        return (
            pltpu.make_async_copy(master_ref.at[taken], master_vmem.at[:, at(step)], master_sem.at[step]),
            pltpu.make_async_copy(second_ref.at[taken], second_vmem.at[:, at(step)], second_sem.at[step]),
        )

    def copy_out(step):
        return pltpu.make_async_copy(out_vmem.at[at(step)], out_ref.at[at(step)], out_sem.at[step])

    small = (
        pltpu.make_async_copy(router_ref, router_vmem, small_sem.at[0]),
        pltpu.make_async_copy(gain_ref, gain_vmem, small_sem.at[1]),
    )
    for copy in small:
        copy.start()
    for step in range(steps):
        for copy in copies(step):
            copy.start()
    for copy in small:
        copy.wait()
    router = (router_vmem[...] * gain_vmem[...]).astype(jnp.bfloat16)
    tile = jnp.concatenate([router, jnp.zeros((TILE - router.shape[0], lanes), jnp.bfloat16)], axis=0)
    for step in range(steps):
        for copy in copies(step):
            copy.wait()
        for s in range(sum(PACK_GROUPS[:step]), sum(PACK_GROUPS[:step + 1])):
            for expert in range(experts):
                out_vmem[s, pl.ds(expert * rows, rows)] = merged(master_vmem[expert, s], second_vmem[expert, s])
            out_vmem[s, pl.ds(experts * rows, TILE)] = tile
        copy_out(step).start()
    for step in range(steps):
        copy_out(step).wait()


def packed(master, second, router, gain, rows):
    experts, shards, _, lanes = master.shape
    steps = len(PACK_GROUPS)
    block = (shards, experts * rows + TILE, lanes)
    return pl.pallas_call(
        packed_kernel,
        in_specs=[pl.BlockSpec(memory_space=pltpu.HBM)] * 4,
        out_specs=pl.BlockSpec(memory_space=pltpu.HBM),
        out_shape=pltpu.HBM(block, jnp.bfloat16),
        scratch_shapes=[
            pltpu.VMEM((experts, shards, rows, lanes), jnp.float32),
            pltpu.VMEM((experts, shards, rows, lanes), jnp.bfloat16),
            pltpu.VMEM(router.shape, jnp.float32),
            pltpu.VMEM(gain.shape, jnp.float32),
            pltpu.VMEM(block, jnp.bfloat16),
            pltpu.SemaphoreType.DMA((steps,)),
            pltpu.SemaphoreType.DMA((steps,)),
            pltpu.SemaphoreType.DMA((steps,)),
            pltpu.SemaphoreType.DMA((2,)),
        ],
        compiler_params=pltpu.CompilerParams(vmem_limit_bytes=VMEM_LIMIT),
        name="packed",
    )(master, second, pltpu.with_memory_space_constraint(router, pltpu.HBM), pltpu.with_memory_space_constraint(gain, pltpu.HBM))


def sorted_kernel(targets, master_ref, second_ref, *refs):
    outs = refs[:CROSS]
    master_vmem, second_vmem, out_vmem, master_sem, second_sem, out_sem = refs[CROSS:]
    experts, shards, rows, _ = master_vmem.shape
    first = master_ref.shape[2] - rows

    def copies(s):
        taken = (slice(None), targets[s], pl.ds(first, rows))
        return (
            pltpu.make_async_copy(master_ref.at[taken], master_vmem.at[:, s], master_sem.at[s]),
            pltpu.make_async_copy(second_ref.at[taken], second_vmem.at[:, s], second_sem.at[s]),
        )

    def copy_out(i):
        return pltpu.make_async_copy(out_vmem.at[i], outs[i], out_sem.at[i])

    for s in range(shards):
        for copy in copies(s):
            copy.start()
    for i in range(CROSS):
        for j in range(RING):
            for copy in copies(i * RING + j):
                copy.wait()
            for expert in range(experts):
                out_vmem[i, j, pl.ds(expert * rows, rows)] = merged(
                    master_vmem[expert, i * RING + j], second_vmem[expert, i * RING + j]
                )
        copy_out(i).start()
    for i in range(CROSS):
        copy_out(i).wait()


def sorted_by_cross(targets, master, second, rows):
    experts, shards, _, lanes = master.shape
    block = (RING, experts * rows, lanes)
    return pl.pallas_call(
        sorted_kernel,
        in_specs=[pl.BlockSpec(memory_space=pltpu.SMEM)] + [pl.BlockSpec(memory_space=pltpu.HBM)] * 2,
        out_specs=[pl.BlockSpec(memory_space=pltpu.HBM)] * CROSS,
        out_shape=[pltpu.HBM(block, jnp.bfloat16)] * CROSS,
        scratch_shapes=[
            pltpu.VMEM((experts, shards, rows, lanes), jnp.float32),
            pltpu.VMEM((experts, shards, rows, lanes), jnp.bfloat16),
            pltpu.VMEM((CROSS, *block), jnp.bfloat16),
            pltpu.SemaphoreType.DMA((shards,)),
            pltpu.SemaphoreType.DMA((shards,)),
            pltpu.SemaphoreType.DMA((CROSS,)),
        ],
        compiler_params=pltpu.CompilerParams(vmem_limit_bytes=VMEM_LIMIT),
        name="sorted",
    )(targets, master, second)


def turned_kernel(*refs):
    parts, outs, sems = refs[:CROSS], refs[CROSS:-1], refs[-1]
    copies = [
        pltpu.make_async_copy(parts[i].at[1 + j], out.at[i], sems.at[j, i])
        for j, out in enumerate(outs[1:])
        for i in range(CROSS)
    ]
    for copy in copies:
        copy.start()
    for i in range(CROSS):
        outs[0][i] = parts[i][0]
    for copy in copies:
        copy.wait()


def turned(parts):
    ring, rows, lanes = parts[0].shape
    block = (CROSS, rows, lanes)
    return pl.pallas_call(
        turned_kernel,
        in_specs=[pl.BlockSpec(memory_space=pltpu.VMEM)] * CROSS,
        out_specs=[pl.BlockSpec(memory_space=pltpu.VMEM)] + [pl.BlockSpec(memory_space=pltpu.HBM)] * (ring - 1),
        out_shape=[pltpu.VMEM(block, jnp.bfloat16)] + [pltpu.HBM(block, jnp.bfloat16)] * (ring - 1),
        scratch_shapes=[pltpu.SemaphoreType.DMA((ring - 1, CROSS))],
        compiler_params=pltpu.CompilerParams(vmem_limit_bytes=VMEM_LIMIT),
        name="turned",
    )(*[pltpu.with_memory_space_constraint(part, pltpu.VMEM) for part in parts])


def row_total(parts):
    total = jnp.zeros(parts[0]().shape, jnp.float32)
    for part in parts:
        part = part().astype(jnp.float32)
        total = total + part * part
    return total


def inverse_scale(total):
    return jnp.broadcast_to(1.0 / jnp.sqrt(jnp.sum(total, axis=1, keepdims=True)), total.shape)


def first_kernel(parts_ref, out_ref, total_ref, out_vmem, sems):
    shards, _, lanes = parts_ref.shape
    experts, rows, _ = total_ref.shape
    blocks = rows // NORM_ROWS

    def copy(expert, block):
        at = (expert, pl.ds(block * NORM_ROWS, NORM_ROWS))
        return pltpu.make_async_copy(out_vmem.at[at], out_ref.at[at], sems.at[expert * blocks + block])

    for expert in range(experts):
        for block in range(blocks):
            at = pl.ds(block * NORM_ROWS, NORM_ROWS)
            taken = pl.ds(expert * rows + block * NORM_ROWS, NORM_ROWS)
            total = row_total([lambda s=s: parts_ref[s, taken] for s in range(shards)])
            total_ref[expert, at] = total
            inverse = inverse_scale(total)
            for s in range(shards):
                part = parts_ref[s, taken].astype(jnp.float32)
                out_vmem[expert, at, pl.ds(s * lanes, lanes)] = (part * inverse).astype(jnp.bfloat16)
            copy(expert, block).start()
    for expert in range(experts):
        for block in range(blocks):
            copy(expert, block).wait()


def first_normed(parts, experts, rows, full_rows):
    shards, _, lanes = parts.shape
    width = shards * lanes
    return pl.pallas_call(
        first_kernel,
        in_specs=[pl.BlockSpec(memory_space=pltpu.VMEM)],
        out_specs=[pl.BlockSpec(memory_space=pltpu.HBM), pl.BlockSpec(memory_space=pltpu.VMEM)],
        out_shape=[
            pltpu.HBM((experts, full_rows, width), jnp.bfloat16),
            pltpu.VMEM((experts, rows, lanes), jnp.float32),
        ],
        scratch_shapes=[
            pltpu.VMEM((experts, rows, width), jnp.bfloat16),
            pltpu.SemaphoreType.DMA((experts * rows // NORM_ROWS,)),
        ],
        compiler_params=pltpu.CompilerParams(vmem_limit_bytes=VMEM_LIMIT),
        name="first",
    )(pltpu.with_memory_space_constraint(parts, pltpu.VMEM))


def router_kernel(parts_ref, out_ref, router_vmem, sems):
    shards, rows, lanes = parts_ref.shape
    for s in range(shards):
        router_vmem[:, pl.ds(s * lanes, lanes)] = parts_ref[s, pl.ds(rows - TILE, TILE)][:router_vmem.shape[0]]
    copies = [pltpu.make_async_copy(router_vmem, out_ref.at[i], sems.at[i]) for i in range(out_ref.shape[0])]
    for copy in copies:
        copy.start()
    for copy in copies:
        copy.wait()


def router_copies(parts, columns, count):
    shards, _, lanes = parts.shape
    return pl.pallas_call(
        router_kernel,
        in_specs=[pl.BlockSpec(memory_space=pltpu.VMEM)],
        out_specs=pl.BlockSpec(memory_space=pltpu.HBM),
        out_shape=pltpu.HBM((count, columns, shards * lanes), jnp.bfloat16),
        scratch_shapes=[
            pltpu.VMEM((columns, shards * lanes), jnp.bfloat16),
            pltpu.SemaphoreType.DMA((count,)),
        ],
        compiler_params=pltpu.CompilerParams(vmem_limit_bytes=VMEM_LIMIT),
        name="router",
    )(pltpu.with_memory_space_constraint(parts, pltpu.VMEM))


def last_kernel(first_ref, *refs):
    parts = refs[:RING]
    out_ref, scale_ref, out_vmem, total_vmem, scale_vmem, sems, scale_sem = refs[RING + 1:]
    experts, rows, _ = out_vmem.shape
    first, lanes = first_ref.shape[1:]

    me = lax.axis_index("shard")
    z, c = me >> 2, me & (CROSS - 1)

    def column(j, i):
        place = (((z - j) & (RING - 1)) << 2) | ((c - i) & (CROSS - 1))
        return pl.ds(pl.multiple_of(place * lanes, lanes), lanes)

    def copy(expert):
        return pltpu.make_async_copy(out_vmem.at[expert], out_ref.at[expert, pl.ds(first, rows)], sems.at[expert])

    scale_copy = pltpu.make_async_copy(scale_vmem, scale_ref, scale_sem)
    for expert in range(experts):
        at = pl.ds(expert * rows, rows)
        total = row_total([lambda j=j, i=i: parts[j][i, at] for j in range(RING) for i in range(CROSS)])
        total_vmem[expert, pl.ds(0, first)] = first_ref[expert]
        total_vmem[expert, pl.ds(first, rows)] = total
        inverse = inverse_scale(total)
        for j in range(RING):
            for i in range(CROSS):
                part = parts[j][i, at].astype(jnp.float32)
                out_vmem[expert, :, column(j, i)] = (part * inverse).astype(jnp.bfloat16)
        copy(expert).start()
    for expert in range(experts):
        scale_vmem[pl.ds(expert, 1)] = jnp.sqrt(jnp.sum(jnp.transpose(total_vmem[expert]), axis=0, keepdims=True))
    scale_copy.start()
    for expert in range(experts):
        copy(expert).wait()
    scale_copy.wait()


def last_normed(totals, parts, final):
    experts, full_rows, width = final.shape
    rows, lanes = full_rows - totals.shape[1], totals.shape[2]
    return pl.pallas_call(
        last_kernel,
        in_specs=[pl.BlockSpec(memory_space=pltpu.VMEM)] * (1 + RING)
        + [pl.BlockSpec(memory_space=pltpu.HBM)],
        out_specs=[pl.BlockSpec(memory_space=pltpu.HBM)] * 2,
        out_shape=[
            pltpu.HBM(final.shape, jnp.bfloat16),
            pltpu.HBM((experts, full_rows), jnp.float32),
        ],
        scratch_shapes=[
            pltpu.VMEM((experts, rows, width), jnp.bfloat16),
            pltpu.VMEM((experts, full_rows, lanes), jnp.float32),
            pltpu.VMEM((experts, full_rows), jnp.float32),
            pltpu.SemaphoreType.DMA((experts,)),
            pltpu.SemaphoreType.DMA,
        ],
        input_output_aliases={1 + RING: 0},
        compiler_params=pltpu.CompilerParams(vmem_limit_bytes=VMEM_LIMIT),
        name="last",
    )(*[pltpu.with_memory_space_constraint(x, pltpu.VMEM) for x in (totals, *parts)], final)


def moved(x, dz, dx):
    pairs = [
        (z * CROSS + c, ((z + dz) % RING) * CROSS + (c + dx) % CROSS) for z in range(RING) for c in range(CROSS)
    ]
    return lax.ppermute(x, "shard", pairs)


def body(master_down, second_down, router_weight, router_gain):
    shards = lax.axis_size("shard")
    experts, rows, lanes = master_down.shape
    rows = rows // shards
    cut = (experts, shards, rows, lanes)
    master = pltpu.with_memory_space_constraint(master_down.reshape(cut), pltpu.HBM)
    second = pltpu.with_memory_space_constraint(second_down.reshape(cut), pltpu.HBM)
    me = lax.axis_index("shard")
    z, c = me >> 2, me & (CROSS - 1)
    steps = jnp.arange(shards, dtype=jnp.int32)
    targets = (((z + (steps & (RING - 1))) & (RING - 1)) << 2) | ((c + (steps >> 3)) & (CROSS - 1))
    sent = packed(master, second, router_weight.T, router_gain[None], FIRST_ROWS)
    received = lax.all_to_all(sent, "shard", 0, 0, tiled=True)
    parts = list(sorted_by_cross(targets, master, second, rows - FIRST_ROWS))
    for step in range(1, CROSS):
        parts[step] = moved(parts[step], 0, step)
    blocks = list(turned(parts))
    for step in ALONG:
        blocks[step] = moved(blocks[step], step, 0)
    copies = router_copies(received, router_weight.shape[1], lax.axis_size("expert"))
    gathered = lax.all_to_all(copies, "expert", 0, 0, tiled=True)
    final_down, totals = first_normed(received, experts, FIRST_ROWS, rows)
    serve_router = gathered.reshape(-1, shards * lanes)
    final_down, scale_down = last_normed(totals, blocks, final_down)
    return (final_down, scale_down, serve_router.T)


def solution(mesh):
    placed = (
        P("expert", None, "shard"),
        P("expert", None, "shard"),
        P("shard", "expert"),
        P("shard"),
    )
    return jax.shard_map(
        body,
        mesh=mesh,
        in_specs=placed,
        out_specs=(P("expert", "shard", None), P("expert", "shard"), P()),
        check_vma=False,
    )
```

profile of v0, /device:TPU:6, one launch (start us, length us, event | category | flops | bytes accessed | tf_op | source)
XLA Modules:
  0.0 92.8 jit_solution(8038159173840692570)
XLA Ops:
  0.6 3.7 %packed.1 = bf16[32,264,128]{2,1,0:T(8,128)(2,1)} custom-call(f32[2,32,200,128]{3,2,1,0:T(8,128)} %bitcast.5, bf16[2,32,200,128]{3,2,1,0:T(8,128)(2,1)} %bitcast.7, f32[2,128]{1,0:T(2,128)} %bitcast.10, f32[1,128]{1,0:T(1,128)} %bitcast.11), custom_call_target="tpu_custom_call" | custom-call | tf_op jit(solution)/shard_map/packed/pallas_call | solution.py:71
  4.3 11.6 %all-to-all-start = ((bf16[32,264,128]{2,1,0:T(8,128)(2,1)}), bf16[32,264,128]{2,1,0:T(8,128)(2,1)S(1)}, u32[]{:S(2)}, u32[]{:S(2)}) async-start(bf16[32,264,128]{2,1,0:T(8,128)(2,1)} %packed.1), calls=%async_computation | async-start | bytes 4325376 | tf_op jit(solution)/shard_map/all_to_all | solution.py:338
  15.9 3.9 %sorted.1 = (bf16[8,144,128]{2,1,0:T(8,128)(2,1)}, bf16[8,144,128]{2,1,0:T(8,128)(2,1)}, bf16[8,144,128]{2,1,0:T(8,128)(2,1)}, bf16[8,144,128]{2,1,0:T(8,128)(2,1)}) custom-call(s32[32]{0:T(128)S(1)} %and_or_fusion.targets, f32[2,32,200,128]{3,2,1,0:T(8,128)} %bitcast.6, bf16[2,32,200,128]{3,2,1,0:T(8,128)(2,1)} %bitcast.8), custom_call_target="tpu_custom_call" | custom-call | tf_op jit(solution)/shard_map/sorted/pallas_call | solution.py:127
  19.9 0.3 collective-permute-start
  20.2 2.7 %collective-permute-start.1 = (bf16[8,144,128]{2,1,0:T(8,128)(2,1)}, bf16[8,144,128]{2,1,0:T(8,128)(2,1)S(1)}, u32[]{:S(2)}, u32[]{:S(2)}) collective-permute-start(bf16[8,144,128]{2,1,0:T(8,128)(2,1)} %get-tuple-element.22), channel_id=1, source_target_pairs={{0,2},{1,3},{2,0},{3,1},{4,6},{5,7},{6,4},{7,5},{8,10},{9,11},{10,... | collective-permute-start | bytes 884744 | tf_op jit(solution)/shard_map/ppermute | solution.py:323
  22.9 0.0 collective-permute-start.2
  22.9 20.4 %collective-permute-done.refs_1_ = bf16[8,144,128]{2,1,0:T(8,128)(2,1)S(1)} collective-permute-done((bf16[8,144,128]{2,1,0:T(8,128)(2,1)}, bf16[8,144,128]{2,1,0:T(8,128)(2,1)S(1)}, u32[]{:S(2)}, u32[]{:S(2)}) %collective-permute-start) | collective-permute-done | bytes 294944 | tf_op jit(solution)/shard_map/ppermute | solution.py:323
  43.3 0.0 collective-permute-done.1.refs_2_
  43.3 5.0 %collective-permute-done.2.refs_3_ = bf16[8,144,128]{2,1,0:T(8,128)(2,1)S(1)} collective-permute-done((bf16[8,144,128]{2,1,0:T(8,128)(2,1)}, bf16[8,144,128]{2,1,0:T(8,128)(2,1)S(1)}, u32[]{:S(2)}, u32[]{:S(2)}) %collective-permute-start.2) | collective-permute-done | bytes 294944 | tf_op jit(solution)/shard_map/ppermute | solution.py:323
  48.3 0.0 copy-start
  48.3 1.0 %copy-done = bf16[8,144,128]{2,1,0:T(8,128)(2,1)S(1)} copy-done((bf16[8,144,128]{2,1,0:T(8,128)(2,1)S(1)}, bf16[8,144,128]{2,1,0:T(8,128)(2,1)}, u32[]{:S(2)}) %copy-start) | copy-done | bytes 294936
  49.2 1.2 %turned.1 = (bf16[4,144,128]{2,1,0:T(8,128)(2,1)S(1)}, bf16[4,144,128]{2,1,0:T(8,128)(2,1)}, bf16[4,144,128]{2,1,0:T(8,128)(2,1)}, bf16[4,144,128]{2,1,0:T(8,128...) custom-call(bf16[8,144,128]{2,1,0:T(8,128)(2,1)S(1)} %copy-done, ...), custom_call_target="tpu_custom_call" | custom-call | tf_op jit(solution)/shard_map/turned/pallas_call | solution.py:163
  50.5 1.8 %collective-permute-start.3 = (bf16[4,144,128]{2,1,0:T(8,128)(2,1)}, bf16[4,144,128]{2,1,0:T(8,128)(2,1)S(1)}, u32[]{:S(2)}, u32[]{:S(2)}) collective-permute-start(bf16[4,144,128]{2,1,0:T(8,128)(2,1)} %get-tuple-element.25), channel_id=1, source_target_pairs={{0,4},{1,5},{2,6},{3,7},{4,8},{5,9},{6,10},{7,11},{8,12},{9,13},{1... | collective-permute-start | bytes 442376 | tf_op jit(solution)/shard_map/ppermute | solution.py:323
  52.3 2.4 %collective-permute-start.4 = (bf16[4,144,128]{2,1,0:T(8,128)(2,1)}, bf16[4,144,128]{2,1,0:T(8,128)(2,1)S(1)}, u32[]{:S(2)}, u32[]{:S(2)}) collective-permute-start(bf16[4,144,128]{2,1,0:T(8,128)(2,1)} %get-tuple-element.26), channel_id=1, source_target_pairs={{0,8},{1,9},{2,10},{3,11},{4,12},{5,13},{6,14},{7,15},{8,16},{9,17... | collective-permute-start | bytes 442376 | tf_op jit(solution)/shard_map/ppermute | solution.py:323
  54.7 3.8 %collective-permute-start.5 = (bf16[4,144,128]{2,1,0:T(8,128)(2,1)}, bf16[4,144,128]{2,1,0:T(8,128)(2,1)S(1)}, u32[]{:S(2)}, u32[]{:S(2)}) collective-permute-start(bf16[4,144,128]{2,1,0:T(8,128)(2,1)} %get-tuple-element.27), channel_id=1, source_target_pairs={{0,12},{1,13},{2,14},{3,15},{4,16},{5,17},{6,18},{7,19},{8,20},{9,... | collective-permute-start | bytes 442376 | tf_op jit(solution)/shard_map/ppermute | solution.py:323
  58.5 1.8 %collective-permute-start.6 = (bf16[4,144,128]{2,1,0:T(8,128)(2,1)}, bf16[4,144,128]{2,1,0:T(8,128)(2,1)S(1)}, u32[]{:S(2)}, u32[]{:S(2)}) collective-permute-start(bf16[4,144,128]{2,1,0:T(8,128)(2,1)} %get-tuple-element.28), channel_id=1, source_target_pairs={{0,16},{1,17},{2,18},{3,19},{4,20},{5,21},{6,22},{7,23},{8,24},{9,... | collective-permute-start | bytes 442376 | tf_op jit(solution)/shard_map/ppermute | solution.py:323
  60.3 3.2 %collective-permute-start.7 = (bf16[4,144,128]{2,1,0:T(8,128)(2,1)}, bf16[4,144,128]{2,1,0:T(8,128)(2,1)S(1)}, u32[]{:S(2)}, u32[]{:S(2)}) collective-permute-start(bf16[4,144,128]{2,1,0:T(8,128)(2,1)} %get-tuple-element.29), channel_id=1, source_target_pairs={{0,20},{1,21},{2,22},{3,23},{4,24},{5,25},{6,26},{7,27},{8,28},{9,... | collective-permute-start | bytes 442376 | tf_op jit(solution)/shard_map/ppermute | solution.py:323
  63.6 6.4 %collective-permute-done.3.refs_1_ = bf16[4,144,128]{2,1,0:T(8,128)(2,1)S(1)} collective-permute-done((bf16[4,144,128]{2,1,0:T(8,128)(2,1)}, bf16[4,144,128]{2,1,0:T(8,128)(2,1)S(1)}, u32[]{:S(2)}, u32[]{:S(2)}) %collective-permute-start.3) | collective-permute-done | bytes 147488 | tf_op jit(solution)/shard_map/ppermute | solution.py:323
  70.0 1.7 %collective-permute-start.8 = (bf16[4,144,128]{2,1,0:T(8,128)(2,1)}, bf16[4,144,128]{2,1,0:T(8,128)(2,1)S(1)}, u32[]{:S(2)}, u32[]{:S(2)}) collective-permute-start(bf16[4,144,128]{2,1,0:T(8,128)(2,1)} %get-tuple-element.30), channel_id=1, source_target_pairs={{0,24},{1,25},{2,26},{3,27},{4,28},{5,29},{6,30},{7,31},{8,0},{9,1... | collective-permute-start | bytes 442376 | tf_op jit(solution)/shard_map/ppermute | solution.py:323
  71.6 5.8 %collective-permute-done.4.refs_2_ = bf16[4,144,128]{2,1,0:T(8,128)(2,1)S(1)} collective-permute-done((bf16[4,144,128]{2,1,0:T(8,128)(2,1)}, bf16[4,144,128]{2,1,0:T(8,128)(2,1)S(1)}, u32[]{:S(2)}, u32[]{:S(2)}) %collective-permute-start.4) | collective-permute-done | bytes 147488 | tf_op jit(solution)/shard_map/ppermute | solution.py:323
  77.5 0.7 collective-permute-start.9
  78.2 0.0 all-to-all-done.parts_ref
  78.2 0.7 router.1
  78.9 4.5 %all-to-all-start.1 = ((bf16[8,2,4096]{2,1,0:T(2,128)(2,1)}), bf16[8,2,4096]{2,1,0:T(2,128)(2,1)S(1)}, u32[]{:S(2)}, u32[]{:S(2)}) async-start(bf16[8,2,4096]{2,1,0:T(2,128)(2,1)} %router.1), calls=%async_computation.1 | async-start | bytes 262144 | tf_op jit(solution)/shard_map/all_to_all | solution.py:346
  83.4 1.8 %first.1 = (bf16[2,200,4096]{2,1,0:T(8,128)(2,1)}, f32[2,128,128]{2,1,0:T(8,128)S(1)}) custom-call(bf16[32,264,128]{2,1,0:T(8,128)(2,1)S(1)} %all-to-all-done.parts_ref), custom_call_target="tpu_custom_call" | custom-call | tf_op jit(solution)/shard_map/first/pallas_call | solution.py:214
  85.2 0.8 collective-permute-done.5.refs_3_
  86.1 4.7 %collective-permute-done.6.refs_4_ = bf16[4,144,128]{2,1,0:T(8,128)(2,1)S(1)} collective-permute-done((bf16[4,144,128]{2,1,0:T(8,128)(2,1)}, bf16[4,144,128]{2,1,0:T(8,128)(2,1)S(1)}, u32[]{:S(2)}, u32[]{:S(2)}) %collective-permute-start.6) | collective-permute-done | bytes 147488 | tf_op jit(solution)/shard_map/ppermute | solution.py:323
  90.7 0.0 collective-permute-done.7.refs_5_
  90.7 0.0 collective-permute-done.8.refs_6_
  90.7 0.0 collective-permute-done.9.refs_7_
  90.7 1.3 %last.1 = (bf16[2,200,4096]{2,1,0:T(8,128)(2,1)}, f32[2,200]{1,0:T(2,128)}) custom-call(f32[2,128,128]{2,1,0:T(8,128)S(1)} %get-tuple-element.19.first_ref, bf16[4,144,128]{2,1,0:T(8,128)(2,1)S(1)} %get-tuple-element.24.refs_0_, bf16[4,144,128]{2,1,0:T(8,128)(2,1)S(1)} %collective-permute-done.3.refs_1_, ...), custom_call_target="tpu_custom_call", output_to_operand_aliasing={{0}: (9, {})} | custom-call | tf_op jit(solution)/shard_map/last/pallas_call | solution.py:297
  92.1 0.0 all-to-all-done.1
  92.1 0.7 reshape.17
  (1 shorter events, 0.0 us)
Async XLA Ops:
  4.3 73.9 %all-to-all-start = ((bf16[32,264,128]{2,1,0:T(8,128)(2,1)}), bf16[32,264,128]{2,1,0:T(8,128)(2,1)S(1)}, u32[]{:S(2)}, u32[]{:S(2)}) async-start(bf16[32,264,128]{2,1,0:T(8,128)(2,1)} %packed.1), calls=%async_computation | async-start | bytes 4325376 | tf_op jit(solution)/shard_map/all_to_all | solution.py:338
  19.9 23.5 %collective-permute-start = (bf16[8,144,128]{2,1,0:T(8,128)(2,1)}, bf16[8,144,128]{2,1,0:T(8,128)(2,1)S(1)}, u32[]{:S(2)}, u32[]{:S(2)}) collective-permute-start(bf16[8,144,128]{2,1,0:T(8,128)(2,1)} %get-tuple-element.21), channel_id=1, source_target_pairs={{0,1},{1,2},{2,3},{3,0},{4,5},{5,6},{6,7},{7,4},{8,9},{9,10},{10,1... | collective-permute-start | bytes 884744 | tf_op jit(solution)/shard_map/ppermute | solution.py:323
  20.2 23.1 %collective-permute-start.1 = (bf16[8,144,128]{2,1,0:T(8,128)(2,1)}, bf16[8,144,128]{2,1,0:T(8,128)(2,1)S(1)}, u32[]{:S(2)}, u32[]{:S(2)}) collective-permute-start(bf16[8,144,128]{2,1,0:T(8,128)(2,1)} %get-tuple-element.22), channel_id=1, source_target_pairs={{0,2},{1,3},{2,0},{3,1},{4,6},{5,7},{6,4},{7,5},{8,10},{9,11},{10,... | collective-permute-start | bytes 884744 | tf_op jit(solution)/shard_map/ppermute | solution.py:323
  22.9 25.4 %collective-permute-start.2 = (bf16[8,144,128]{2,1,0:T(8,128)(2,1)}, bf16[8,144,128]{2,1,0:T(8,128)(2,1)S(1)}, u32[]{:S(2)}, u32[]{:S(2)}) collective-permute-start(bf16[8,144,128]{2,1,0:T(8,128)(2,1)} %get-tuple-element.23), channel_id=1, source_target_pairs={{0,3},{1,0},{2,1},{3,2},{4,7},{5,4},{6,5},{7,6},{8,11},{9,8},{10,9... | collective-permute-start | bytes 884744 | tf_op jit(solution)/shard_map/ppermute | solution.py:323
  48.3 1.0 %copy-start = (bf16[8,144,128]{2,1,0:T(8,128)(2,1)S(1)}, bf16[8,144,128]{2,1,0:T(8,128)(2,1)}, u32[]{:S(2)}) copy-start(bf16[8,144,128]{2,1,0:T(8,128)(2,1)} %get-tuple-element.20.refs_0_) | copy-start | bytes 884740
  50.5 19.5 %collective-permute-start.3 = (bf16[4,144,128]{2,1,0:T(8,128)(2,1)}, bf16[4,144,128]{2,1,0:T(8,128)(2,1)S(1)}, u32[]{:S(2)}, u32[]{:S(2)}) collective-permute-start(bf16[4,144,128]{2,1,0:T(8,128)(2,1)} %get-tuple-element.25), channel_id=1, source_target_pairs={{0,4},{1,5},{2,6},{3,7},{4,8},{5,9},{6,10},{7,11},{8,12},{9,13},{1... | collective-permute-start | bytes 442376 | tf_op jit(solution)/shard_map/ppermute | solution.py:323
  52.3 25.2 %collective-permute-start.4 = (bf16[4,144,128]{2,1,0:T(8,128)(2,1)}, bf16[4,144,128]{2,1,0:T(8,128)(2,1)S(1)}, u32[]{:S(2)}, u32[]{:S(2)}) collective-permute-start(bf16[4,144,128]{2,1,0:T(8,128)(2,1)} %get-tuple-element.26), channel_id=1, source_target_pairs={{0,8},{1,9},{2,10},{3,11},{4,12},{5,13},{6,14},{7,15},{8,16},{9,17... | collective-permute-start | bytes 442376 | tf_op jit(solution)/shard_map/ppermute | solution.py:323
  54.7 31.4 %collective-permute-start.5 = (bf16[4,144,128]{2,1,0:T(8,128)(2,1)}, bf16[4,144,128]{2,1,0:T(8,128)(2,1)S(1)}, u32[]{:S(2)}, u32[]{:S(2)}) collective-permute-start(bf16[4,144,128]{2,1,0:T(8,128)(2,1)} %get-tuple-element.27), channel_id=1, source_target_pairs={{0,12},{1,13},{2,14},{3,15},{4,16},{5,17},{6,18},{7,19},{8,20},{9,... | collective-permute-start | bytes 442376 | tf_op jit(solution)/shard_map/ppermute | solution.py:323
  58.5 32.2 %collective-permute-start.6 = (bf16[4,144,128]{2,1,0:T(8,128)(2,1)}, bf16[4,144,128]{2,1,0:T(8,128)(2,1)S(1)}, u32[]{:S(2)}, u32[]{:S(2)}) collective-permute-start(bf16[4,144,128]{2,1,0:T(8,128)(2,1)} %get-tuple-element.28), channel_id=1, source_target_pairs={{0,16},{1,17},{2,18},{3,19},{4,20},{5,21},{6,22},{7,23},{8,24},{9,... | collective-permute-start | bytes 442376 | tf_op jit(solution)/shard_map/ppermute | solution.py:323
  60.3 30.4 %collective-permute-start.7 = (bf16[4,144,128]{2,1,0:T(8,128)(2,1)}, bf16[4,144,128]{2,1,0:T(8,128)(2,1)S(1)}, u32[]{:S(2)}, u32[]{:S(2)}) collective-permute-start(bf16[4,144,128]{2,1,0:T(8,128)(2,1)} %get-tuple-element.29), channel_id=1, source_target_pairs={{0,20},{1,21},{2,22},{3,23},{4,24},{5,25},{6,26},{7,27},{8,28},{9,... | collective-permute-start | bytes 442376 | tf_op jit(solution)/shard_map/ppermute | solution.py:323
  70.0 20.8 %collective-permute-start.8 = (bf16[4,144,128]{2,1,0:T(8,128)(2,1)}, bf16[4,144,128]{2,1,0:T(8,128)(2,1)S(1)}, u32[]{:S(2)}, u32[]{:S(2)}) collective-permute-start(bf16[4,144,128]{2,1,0:T(8,128)(2,1)} %get-tuple-element.30), channel_id=1, source_target_pairs={{0,24},{1,25},{2,26},{3,27},{4,28},{5,29},{6,30},{7,31},{8,0},{9,1... | collective-permute-start | bytes 442376 | tf_op jit(solution)/shard_map/ppermute | solution.py:323
  77.5 13.3 %collective-permute-start.9 = (bf16[4,144,128]{2,1,0:T(8,128)(2,1)}, bf16[4,144,128]{2,1,0:T(8,128)(2,1)S(1)}, u32[]{:S(2)}, u32[]{:S(2)}) collective-permute-start(bf16[4,144,128]{2,1,0:T(8,128)(2,1)} %get-tuple-element.31), channel_id=1, source_target_pairs={{0,28},{1,29},{2,30},{3,31},{4,0},{5,1},{6,2},{7,3},{8,4},{9,5},{1... | collective-permute-start | bytes 442376 | tf_op jit(solution)/shard_map/ppermute | solution.py:323
  78.9 13.2 %all-to-all-start.1 = ((bf16[8,2,4096]{2,1,0:T(2,128)(2,1)}), bf16[8,2,4096]{2,1,0:T(2,128)(2,1)S(1)}, u32[]{:S(2)}, u32[]{:S(2)}) async-start(bf16[8,2,4096]{2,1,0:T(2,128)(2,1)} %router.1), calls=%async_computation.1 | async-start | bytes 262144 | tf_op jit(solution)/shard_map/all_to_all | solution.py:346
where the time goes:
time: 93.5 us; the launch traced here: 92.8 us
  waiting for transfers between devices  43.1 us (46%)
  starting transfers between devices  34.6 us (37%)
  Pallas kernels  12.7 us (14%)
  local copies, waits for them, and re-layouts  1.67 us (2%)
    ppermute x10, waiting for transfers between devices, moved(): return lax.ppermute(x, 'shard', pairs)  43.1 us
    ppermute x10, starting transfers between devices, moved(): return lax.ppermute(x, 'shard', pairs)  18.5 us
    all_to_all x1, starting transfers between devices, body(): received = lax.all_to_all(sent, 'shard', 0, 0, tiled=True)  11.6 us
    all_to_all x1, starting transfers between devices, body(): gathered = lax.all_to_all(copies, 'expert', 0, 0, tiled=True)  4.48 us
    pallas_call x1, Pallas kernels, sorted_by_cross(): pl.pallas_call(sorted_kernel, in_specs=[pl.BlockSpec(memory_space=pltpu.S...  3.95 us
    pallas_call x1, Pallas kernels, packed(): pl.pallas_call(packed_kernel, in_specs=[pl.BlockSpec(memory_space=pltpu.H...  3.67 us
  transfers between devices with their start and end apart: 12, of which 6 were waited for; matrix products, arithmetic and copies ran while one was open for 0% of the time, Pallas kernels for 10%

commit v1 on v0

--- a/solution.py
+++ b/solution.py
@@ -9,7 +9,6 @@
 RING, CROSS = 8, 4
 FIRST_ROWS = 128
 PACK_GROUPS = (16, 8, 4, 4)
-TILE = 8
 NORM_ROWS = 32
 VMEM_LIMIT = 32 << 20
 ALONG = (4, 3, 5, 2, 6, 1, 7)
@@ -19,11 +18,8 @@
     return (master + second.astype(jnp.float32)).astype(jnp.bfloat16)
 
 
-def packed_kernel(
-    master_ref, second_ref, router_ref, gain_ref, out_ref,
-    master_vmem, second_vmem, router_vmem, gain_vmem, out_vmem, master_sem, second_sem, out_sem, small_sem,
-):
-    experts, _, rows, lanes = master_vmem.shape
+def packed_kernel(master_ref, second_ref, out_ref, master_vmem, second_vmem, out_vmem, master_sem, second_sem, out_sem):
+    rows = out_ref.shape[2]
     steps = len(PACK_GROUPS)
 
     def at(step):
@@ -39,54 +35,38 @@
     def copy_out(step):
         return pltpu.make_async_copy(out_vmem.at[at(step)], out_ref.at[at(step)], out_sem.at[step])
 
-    small = (
-        pltpu.make_async_copy(router_ref, router_vmem, small_sem.at[0]),
-        pltpu.make_async_copy(gain_ref, gain_vmem, small_sem.at[1]),
-    )
-    for copy in small:
-        copy.start()
     for step in range(steps):
         for copy in copies(step):
             copy.start()
-    for copy in small:
-        copy.wait()
-    router = (router_vmem[...] * gain_vmem[...]).astype(jnp.bfloat16)
-    tile = jnp.concatenate([router, jnp.zeros((TILE - router.shape[0], lanes), jnp.bfloat16)], axis=0)
     for step in range(steps):
         for copy in copies(step):
             copy.wait()
         for s in range(sum(PACK_GROUPS[:step]), sum(PACK_GROUPS[:step + 1])):
-            for expert in range(experts):
-                out_vmem[s, pl.ds(expert * rows, rows)] = merged(master_vmem[expert, s], second_vmem[expert, s])
-            out_vmem[s, pl.ds(experts * rows, TILE)] = tile
+            out_vmem[s] = merged(master_vmem[:, s], second_vmem[:, s])
         copy_out(step).start()
     for step in range(steps):
         copy_out(step).wait()
 
 
-def packed(master, second, router, gain, rows):
+def packed(master, second, rows):
     experts, shards, _, lanes = master.shape
     steps = len(PACK_GROUPS)
-    block = (shards, experts * rows + TILE, lanes)
     return pl.pallas_call(
         packed_kernel,
-        in_specs=[pl.BlockSpec(memory_space=pltpu.HBM)] * 4,
+        in_specs=[pl.BlockSpec(memory_space=pltpu.HBM)] * 2,
         out_specs=pl.BlockSpec(memory_space=pltpu.HBM),
-        out_shape=pltpu.HBM(block, jnp.bfloat16),
+        out_shape=pltpu.HBM((shards, experts, rows, lanes), jnp.bfloat16),
         scratch_shapes=[
             pltpu.VMEM((experts, shards, rows, lanes), jnp.float32),
             pltpu.VMEM((experts, shards, rows, lanes), jnp.bfloat16),
-            pltpu.VMEM(router.shape, jnp.float32),
-            pltpu.VMEM(gain.shape, jnp.float32),
-            pltpu.VMEM(block, jnp.bfloat16),
+            pltpu.VMEM((shards, experts, rows, lanes), jnp.bfloat16),
             pltpu.SemaphoreType.DMA((steps,)),
             pltpu.SemaphoreType.DMA((steps,)),
             pltpu.SemaphoreType.DMA((steps,)),
-            pltpu.SemaphoreType.DMA((2,)),
         ],
         compiler_params=pltpu.CompilerParams(vmem_limit_bytes=VMEM_LIMIT),
         name="packed",
-    )(master, second, pltpu.with_memory_space_constraint(router, pltpu.HBM), pltpu.with_memory_space_constraint(gain, pltpu.HBM))
+    )(master, second)
 
 
 def sorted_kernel(targets, master_ref, second_ref, *refs):
@@ -184,8 +164,7 @@
 
 
 def first_kernel(parts_ref, out_ref, total_ref, out_vmem, sems):
-    shards, _, lanes = parts_ref.shape
-    experts, rows, _ = total_ref.shape
+    shards, experts, rows, lanes = parts_ref.shape
     blocks = rows // NORM_ROWS
 
     def copy(expert, block):
@@ -195,12 +174,11 @@
     for expert in range(experts):
         for block in range(blocks):
             at = pl.ds(block * NORM_ROWS, NORM_ROWS)
-            taken = pl.ds(expert * rows + block * NORM_ROWS, NORM_ROWS)
-            total = row_total([lambda s=s: parts_ref[s, taken] for s in range(shards)])
+            total = row_total([lambda s=s: parts_ref[s, expert, at] for s in range(shards)])
             total_ref[expert, at] = total
             inverse = inverse_scale(total)
             for s in range(shards):
-                part = parts_ref[s, taken].astype(jnp.float32)
+                part = parts_ref[s, expert, at].astype(jnp.float32)
                 out_vmem[expert, at, pl.ds(s * lanes, lanes)] = (part * inverse).astype(jnp.bfloat16)
             copy(expert, block).start()
     for expert in range(experts):
@@ -208,8 +186,8 @@
             copy(expert, block).wait()
 
 
-def first_normed(parts, experts, rows, full_rows):
-    shards, _, lanes = parts.shape
+def first_normed(parts, full_rows):
+    shards, experts, rows, lanes = parts.shape
     width = shards * lanes
     return pl.pallas_call(
         first_kernel,
@@ -228,10 +206,21 @@
     )(pltpu.with_memory_space_constraint(parts, pltpu.VMEM))
 
 
-def router_kernel(parts_ref, out_ref, router_vmem, sems):
-    shards, rows, lanes = parts_ref.shape
-    for s in range(shards):
-        router_vmem[:, pl.ds(s * lanes, lanes)] = parts_ref[s, pl.ds(rows - TILE, TILE)][:router_vmem.shape[0]]
+def column_at(j, i, lanes):
+    me = lax.axis_index("shard")
+    z, c = me >> 2, me & (CROSS - 1)
+    place = (((z - j) & (RING - 1)) << 2) | ((c - i) & (CROSS - 1))
+    return pl.ds(pl.multiple_of(place * lanes, lanes), lanes)
+
+
+def router_kernel(*refs):
+    tiles, (out_ref, router_vmem, sems) = refs[:RING], refs[RING:]
+    columns = router_vmem.shape[0]
+    lanes = tiles[0].shape[1]
+    for j in range(RING):
+        tile = tiles[j][...]
+        for i in range(CROSS):
+            router_vmem[:, column_at(j, i, lanes)] = tile[i * columns:(i + 1) * columns]
     copies = [pltpu.make_async_copy(router_vmem, out_ref.at[i], sems.at[i]) for i in range(out_ref.shape[0])]
     for copy in copies:
         copy.start()
@@ -239,20 +228,21 @@
         copy.wait()
 
 
-def router_copies(parts, columns, count):
-    shards, _, lanes = parts.shape
+def router_copies(tiles, count):
+    columns, lanes = tiles[0].shape[0] // CROSS, tiles[0].shape[1]
+    width = RING * CROSS * lanes
     return pl.pallas_call(
         router_kernel,
-        in_specs=[pl.BlockSpec(memory_space=pltpu.VMEM)],
+        in_specs=[pl.BlockSpec(memory_space=pltpu.VMEM)] * RING,
         out_specs=pl.BlockSpec(memory_space=pltpu.HBM),
-        out_shape=pltpu.HBM((count, columns, shards * lanes), jnp.bfloat16),
-        scratch_shapes=[
-            pltpu.VMEM((columns, shards * lanes), jnp.bfloat16),
+        out_shape=pltpu.HBM((count, columns, width), jnp.bfloat16),
+        scratch_shapes=[
+            pltpu.VMEM((columns, width), jnp.bfloat16),
             pltpu.SemaphoreType.DMA((count,)),
         ],
         compiler_params=pltpu.CompilerParams(vmem_limit_bytes=VMEM_LIMIT),
         name="router",
-    )(pltpu.with_memory_space_constraint(parts, pltpu.VMEM))
+    )(*[pltpu.with_memory_space_constraint(tile, pltpu.VMEM) for tile in tiles])
 
 
 def last_kernel(first_ref, *refs):
@@ -261,12 +251,8 @@
     experts, rows, _ = out_vmem.shape
     first, lanes = first_ref.shape[1:]
 
-    me = lax.axis_index("shard")
-    z, c = me >> 2, me & (CROSS - 1)
-
     def column(j, i):
-        place = (((z - j) & (RING - 1)) << 2) | ((c - i) & (CROSS - 1))
-        return pl.ds(pl.multiple_of(place * lanes, lanes), lanes)
+        return column_at(j, i, lanes)
 
     def copy(expert):
         return pltpu.make_async_copy(out_vmem.at[expert], out_ref.at[expert, pl.ds(first, rows)], sems.at[expert])
@@ -334,17 +320,24 @@
     z, c = me >> 2, me & (CROSS - 1)
     steps = jnp.arange(shards, dtype=jnp.int32)
     targets = (((z + (steps & (RING - 1))) & (RING - 1)) << 2) | ((c + (steps >> 3)) & (CROSS - 1))
-    sent = packed(master, second, router_weight.T, router_gain[None], FIRST_ROWS)
+    sent = packed(master, second, FIRST_ROWS)
     received = lax.all_to_all(sent, "shard", 0, 0, tiled=True)
+    pieces = [(router_weight * router_gain[:, None]).astype(jnp.bfloat16).T]
+    for step in range(1, CROSS):
+        pieces.append(moved(pieces[0], 0, step))
+    tile = jnp.concatenate(pieces, axis=0)
+    tiles = [tile] * RING
+    for step in ALONG:
+        tiles[step] = moved(tile, step, 0)
     parts = list(sorted_by_cross(targets, master, second, rows - FIRST_ROWS))
     for step in range(1, CROSS):
         parts[step] = moved(parts[step], 0, step)
     blocks = list(turned(parts))
     for step in ALONG:
         blocks[step] = moved(blocks[step], step, 0)
-    copies = router_copies(received, router_weight.shape[1], lax.axis_size("expert"))
+    copies = router_copies(tiles, lax.axis_size("expert"))
     gathered = lax.all_to_all(copies, "expert", 0, 0, tiled=True)
-    final_down, totals = first_normed(received, experts, FIRST_ROWS, rows)
+    final_down, totals = first_normed(received, rows)
     serve_router = gathered.reshape(-1, shards * lanes)
     final_down, scale_down = last_normed(totals, blocks, final_down)
     return (final_down, scale_down, serve_router.T)

time: 93.5 us -> 123 us (1.32)
  waiting for transfers between devices: 43.1 us -> 59.2 us
  starting transfers between devices: 34.6 us -> 47.5 us
    ppermute x10 -> x20, starting transfers between devices: 18.5 us -> 36.7 us  [moved(): return lax.ppermute(x, 'shard', pairs)]
    ppermute x10 -> x20, waiting for transfers between devices: 43.1 us -> 56.7 us  [moved(): return lax.ppermute(x, 'shard', pairs)]
    all_to_all x1, starting transfers between devices: 11.6 us -> 6.32 us  [body(): received = lax.all_to_all(sent, 'shard', 0, 0, tiled=True)]
    all_to_all x1, waiting for transfers between devices: 0.01 us -> 2.48 us  [body(): gathered = lax.all_to_all(copies, 'expert', 0, 0, tiled=True)]
  transfers between devices with their start and end apart: 12 -> 22, of which waited for: 6 -> 12; matrix products, arithmetic and copies ran while one was open for 0% -> 1% of each run, Pallas kernels for 10% -> 8%
where the time goes in v1:
time: 123 us; the launch traced here: 122 us
  waiting for transfers between devices  59.2 us (48%)
  starting transfers between devices  47.5 us (39%)
  Pallas kernels  12.5 us (10%)
  local copies, waits for them, and re-layouts  1.67 us (1%)
    ppermute x20, waiting for transfers between devices, moved(): return lax.ppermute(x, 'shard', pairs)  56.7 us
    ppermute x20, starting transfers between devices, moved(): return lax.ppermute(x, 'shard', pairs)  36.7 us
    all_to_all x1, starting transfers between devices, body(): received = lax.all_to_all(sent, 'shard', 0, 0, tiled=True)  6.32 us
    all_to_all x1, starting transfers between devices, body(): gathered = lax.all_to_all(copies, 'expert', 0, 0, tiled=True)  4.48 us
    pallas_call x1, Pallas kernels, sorted_by_cross(): pl.pallas_call(sorted_kernel, in_specs=[pl.BlockSpec(memory_space=pltpu.S...  3.95 us
    pallas_call x1, Pallas kernels, packed(): pl.pallas_call(packed_kernel, in_specs=[pl.BlockSpec(memory_space=pltpu.H...  3.61 us
    all_to_all x1, waiting for transfers between devices, body(): gathered = lax.all_to_all(copies, 'expert', 0, 0, tiled=True)  2.48 us
  transfers between devices with their start and end apart: 22, of which 12 were waited for; matrix products, arithmetic and copies ran while one was open for 1% of the time, Pallas kernels for 8%

profile of v1, /device:TPU:6, one launch (start us, length us, event | category | flops | bytes accessed | tf_op | source)
XLA Modules:
  0.0 122.4 jit_solution(16906295561595343772)
XLA Ops:
  0.6 0.7 fusion
  1.3 2.2 %collective-permute-start.10 = (bf16[2,128]{1,0:T(2,128)(2,1)S(1)}, bf16[2,128]{1,0:T(2,128)(2,1)S(1)}, u32[]{:S(2)}, u32[]{:S(2)}) collective-permute-start(bf16[2,128]{1,0:T(2,128)(2,1)S(1)} %fusion), channel_id=1, source_target_pairs={{0,1},{1,2},{2,3},{3,0},{4,5},{5,6},{6,7},{7,4},{8,9},{9,10},{10,1... | collective-permute-start | bytes 1544 | tf_op jit(solution)/shard_map/ppermute | solution.py:309
  3.5 0.7 collective-permute-start.11
  4.2 0.1 collective-permute-start.12
  4.4 0.5 collective-permute-done.10
  4.9 3.7 %collective-permute-done.11 = bf16[2,128]{1,0:T(2,128)(2,1)S(1)} collective-permute-done((bf16[2,128]{1,0:T(2,128)(2,1)S(1)}, bf16[2,128]{1,0:T(2,128)(2,1)S(1)}, u32[]{:S(2)}, u32[]{:S(2)}) %collective-permute-start.11) | collective-permute-done | bytes 544 | tf_op jit(solution)/shard_map/ppermute | solution.py:309
  8.6 0.4 collective-permute-done.12
  9.0 2.0 %collective-permute-start.13 = (bf16[8,128]{1,0:T(8,128)(2,1)S(1)}, bf16[8,128]{1,0:T(8,128)(2,1)S(1)}, u32[]{:S(2)}, u32[]{:S(2)}) collective-permute-start(bf16[8,128]{1,0:T(8,128)(2,1)S(1)} %pad_maximum_fusion.refs_0_), channel_id=1, source_target_pairs={{0,4},{1,5},{2,6},{3,7},{4,8},{5,9},{6,10},{7,11},{8,12},{9,13},{1... | collective-permute-start | bytes 6152 | tf_op jit(solution)/shard_map/ppermute | solution.py:309
  11.0 3.3 %collective-permute-start.14 = (bf16[8,128]{1,0:T(8,128)(2,1)S(1)}, bf16[8,128]{1,0:T(8,128)(2,1)S(1)}, u32[]{:S(2)}, u32[]{:S(2)}) collective-permute-start(bf16[8,128]{1,0:T(8,128)(2,1)S(1)} %pad_maximum_fusion.refs_0_), channel_id=1, source_target_pairs={{0,8},{1,9},{2,10},{3,11},{4,12},{5,13},{6,14},{7,15},{8,16},{9,17... | collective-permute-start | bytes 6152 | tf_op jit(solution)/shard_map/ppermute | solution.py:309
  14.3 4.0 %collective-permute-start.15 = (bf16[8,128]{1,0:T(8,128)(2,1)S(1)}, bf16[8,128]{1,0:T(8,128)(2,1)S(1)}, u32[]{:S(2)}, u32[]{:S(2)}) collective-permute-start(bf16[8,128]{1,0:T(8,128)(2,1)S(1)} %pad_maximum_fusion.refs_0_), channel_id=1, source_target_pairs={{0,12},{1,13},{2,14},{3,15},{4,16},{5,17},{6,18},{7,19},{8,20},{9,... | collective-permute-start | bytes 6152 | tf_op jit(solution)/shard_map/ppermute | solution.py:309
  18.3 0.5 collective-permute-start.16
  18.9 4.9 %collective-permute-start.17 = (bf16[8,128]{1,0:T(8,128)(2,1)S(1)}, bf16[8,128]{1,0:T(8,128)(2,1)S(1)}, u32[]{:S(2)}, u32[]{:S(2)}) collective-permute-start(bf16[8,128]{1,0:T(8,128)(2,1)S(1)} %pad_maximum_fusion.refs_0_), channel_id=1, source_target_pairs={{0,20},{1,21},{2,22},{3,23},{4,24},{5,25},{6,26},{7,27},{8,28},{9,... | collective-permute-start | bytes 6152 | tf_op jit(solution)/shard_map/ppermute | solution.py:309
  23.8 0.0 collective-permute-done.13.refs_1_
  23.8 2.7 %collective-permute-start.18 = (bf16[8,128]{1,0:T(8,128)(2,1)S(1)}, bf16[8,128]{1,0:T(8,128)(2,1)S(1)}, u32[]{:S(2)}, u32[]{:S(2)}) collective-permute-start(bf16[8,128]{1,0:T(8,128)(2,1)S(1)} %pad_maximum_fusion.refs_0_), channel_id=1, source_target_pairs={{0,24},{1,25},{2,26},{3,27},{4,28},{5,29},{6,30},{7,31},{8,0},{9,1... | collective-permute-start | bytes 6152 | tf_op jit(solution)/shard_map/ppermute | solution.py:309
  26.5 0.0 collective-permute-done.14.refs_2_
  26.5 1.0 collective-permute-start.19
  27.5 0.0 collective-permute-done.15.refs_3_
  27.5 0.0 collective-permute-done.16.refs_4_
  27.5 0.0 collective-permute-done.17.refs_5_
  27.5 0.8 collective-permute-done.18.refs_6_
  28.3 1.8 %collective-permute-done.19.refs_7_ = bf16[8,128]{1,0:T(8,128)(2,1)S(1)} collective-permute-done((bf16[8,128]{1,0:T(8,128)(2,1)S(1)}, bf16[8,128]{1,0:T(8,128)(2,1)S(1)}, u32[]{:S(2)}, u32[]{:S(2)}) %collective-permute-start.19) | collective-permute-done | bytes 2080 | tf_op jit(solution)/shard_map/ppermute | solution.py:309
  30.1 0.8 router.1
  30.8 4.5 %all-to-all-start.1 = ((bf16[8,2,4096]{2,1,0:T(2,128)(2,1)}), bf16[8,2,4096]{2,1,0:T(2,128)(2,1)S(1)}, u32[]{:S(2)}, u32[]{:S(2)}) async-start(bf16[8,2,4096]{2,1,0:T(2,128)(2,1)} %router.1), calls=%async_computation.1 | async-start | bytes 262144 | tf_op jit(solution)/shard_map/all_to_all | solution.py:339
  35.3 3.6 %packed.1 = bf16[32,2,128,128]{3,2,1,0:T(8,128)(2,1)} custom-call(f32[2,32,200,128]{3,2,1,0:T(8,128)} %bitcast.5, bf16[2,32,200,128]{3,2,1,0:T(8,128)(2,1)} %bitcast.7), custom_call_target="tpu_custom_call" | custom-call | tf_op jit(solution)/shard_map/packed/pallas_call | solution.py:54
  38.9 2.5 %all-to-all-done.1 = bf16[8,2,4096]{2,1,0:T(2,128)(2,1)S(1)} async-done(((bf16[8,2,4096]{2,1,0:T(2,128)(2,1)}), bf16[8,2,4096]{2,1,0:T(2,128)(2,1)S(1)}, u32[]{:S(2)}, u32[]{:S(2)}) %all-to-all-start.1) | async-done | bytes 131104 | tf_op jit(solution)/shard_map/all_to_all | solution.py:339
  41.4 6.3 %all-to-all-start = ((bf16[32,2,128,128]{3,2,1,0:T(8,128)(2,1)}), bf16[32,2,128,128]{3,2,1,0:T(8,128)(2,1)S(1)}, u32[]{:S(2)}, u32[]{:S(2)}) async-start(bf16[32,2,128,128]{3,2,1,0:T(8,128)(2,1)} %packed.1), calls=%async_computation | async-start | bytes 4194304 | tf_op jit(solution)/shard_map/all_to_all | solution.py:324
  47.8 4.0 %sorted.1 = (bf16[8,144,128]{2,1,0:T(8,128)(2,1)}, bf16[8,144,128]{2,1,0:T(8,128)(2,1)}, bf16[8,144,128]{2,1,0:T(8,128)(2,1)}, bf16[8,144,128]{2,1,0:T(8,128)(2,1)}) custom-call(s32[32]{0:T(128)S(1)} %and_or_fusion.targets, f32[2,32,200,128]{3,2,1,0:T(8,128)} %bitcast.6, bf16[2,32,200,128]{3,2,1,0:T(8,128)(2,1)} %bitcast.8), custom_call_target="tpu_custom_call" | custom-call | tf_op jit(solution)/shard_map/sorted/pallas_call | solution.py:107
  51.7 0.3 collective-permute-start
  52.0 2.7 %collective-permute-start.1 = (bf16[8,144,128]{2,1,0:T(8,128)(2,1)}, bf16[8,144,128]{2,1,0:T(8,128)(2,1)S(1)}, u32[]{:S(2)}, u32[]{:S(2)}) collective-permute-start(bf16[8,144,128]{2,1,0:T(8,128)(2,1)} %get-tuple-element.22), channel_id=1, source_target_pairs={{0,2},{1,3},{2,0},{3,1},{4,6},{5,7},{6,4},{7,5},{8,10},{9,11},{10,... | collective-permute-start | bytes 884744 | tf_op jit(solution)/shard_map/ppermute | solution.py:309
  54.7 0.0 collective-permute-start.2
  54.7 19.5 %collective-permute-done.refs_1_ = bf16[8,144,128]{2,1,0:T(8,128)(2,1)S(1)} collective-permute-done((bf16[8,144,128]{2,1,0:T(8,128)(2,1)}, bf16[8,144,128]{2,1,0:T(8,128)(2,1)S(1)}, u32[]{:S(2)}, u32[]{:S(2)}) %collective-permute-start) | collective-permute-done | bytes 294944 | tf_op jit(solution)/shard_map/ppermute | solution.py:309
  74.3 0.0 collective-permute-done.1.refs_2_
  74.3 8.4 %collective-permute-done.2.refs_3_ = bf16[8,144,128]{2,1,0:T(8,128)(2,1)S(1)} collective-permute-done((bf16[8,144,128]{2,1,0:T(8,128)(2,1)}, bf16[8,144,128]{2,1,0:T(8,128)(2,1)S(1)}, u32[]{:S(2)}, u32[]{:S(2)}) %collective-permute-start.2) | collective-permute-done | bytes 294944 | tf_op jit(solution)/shard_map/ppermute | solution.py:309
  82.7 0.0 copy-start
  82.7 1.0 copy-done
  83.6 1.3 %turned.1 = (bf16[4,144,128]{2,1,0:T(8,128)(2,1)S(1)}, bf16[4,144,128]{2,1,0:T(8,128)(2,1)}, bf16[4,144,128]{2,1,0:T(8,128)(2,1)}, bf16[4,144,128]{2,1,0:T(8,128...) custom-call(bf16[8,144,128]{2,1,0:T(8,128)(2,1)S(1)} %copy-done, ...), custom_call_target="tpu_custom_call" | custom-call | tf_op jit(solution)/shard_map/turned/pallas_call | solution.py:143
  84.9 0.1 collective-permute-start.3
  85.0 1.0 collective-permute-start.4
  86.0 4.2 %collective-permute-start.5 = (bf16[4,144,128]{2,1,0:T(8,128)(2,1)}, bf16[4,144,128]{2,1,0:T(8,128)(2,1)S(1)}, u32[]{:S(2)}, u32[]{:S(2)}) collective-permute-start(bf16[4,144,128]{2,1,0:T(8,128)(2,1)} %get-tuple-element.27), channel_id=1, source_target_pairs={{0,12},{1,13},{2,14},{3,15},{4,16},{5,17},{6,18},{7,19},{8,20},{9,... | collective-permute-start | bytes 442376 | tf_op jit(solution)/shard_map/ppermute | solution.py:309
  90.2 1.5 %collective-permute-start.6 = (bf16[4,144,128]{2,1,0:T(8,128)(2,1)}, bf16[4,144,128]{2,1,0:T(8,128)(2,1)S(1)}, u32[]{:S(2)}, u32[]{:S(2)}) collective-permute-start(bf16[4,144,128]{2,1,0:T(8,128)(2,1)} %get-tuple-element.28), channel_id=1, source_target_pairs={{0,16},{1,17},{2,18},{3,19},{4,20},{5,21},{6,22},{7,23},{8,24},{9,... | collective-permute-start | bytes 442376 | tf_op jit(solution)/shard_map/ppermute | solution.py:309
  91.7 3.3 %collective-permute-start.7 = (bf16[4,144,128]{2,1,0:T(8,128)(2,1)}, bf16[4,144,128]{2,1,0:T(8,128)(2,1)S(1)}, u32[]{:S(2)}, u32[]{:S(2)}) collective-permute-start(bf16[4,144,128]{2,1,0:T(8,128)(2,1)} %get-tuple-element.29), channel_id=1, source_target_pairs={{0,20},{1,21},{2,22},{3,23},{4,24},{5,25},{6,26},{7,27},{8,28},{9,... | collective-permute-start | bytes 442376 | tf_op jit(solution)/shard_map/ppermute | solution.py:309
  95.0 5.2 %collective-permute-done.3.refs_1_ = bf16[4,144,128]{2,1,0:T(8,128)(2,1)S(1)} collective-permute-done((bf16[4,144,128]{2,1,0:T(8,128)(2,1)}, bf16[4,144,128]{2,1,0:T(8,128)(2,1)S(1)}, u32[]{:S(2)}, u32[]{:S(2)}) %collective-permute-start.3) | collective-permute-done | bytes 147488 | tf_op jit(solution)/shard_map/ppermute | solution.py:309
  100.2 1.8 %collective-permute-start.8 = (bf16[4,144,128]{2,1,0:T(8,128)(2,1)}, bf16[4,144,128]{2,1,0:T(8,128)(2,1)S(1)}, u32[]{:S(2)}, u32[]{:S(2)}) collective-permute-start(bf16[4,144,128]{2,1,0:T(8,128)(2,1)} %get-tuple-element.30), channel_id=1, source_target_pairs={{0,24},{1,25},{2,26},{3,27},{4,28},{5,29},{6,30},{7,31},{8,0},{9,1... | collective-permute-start | bytes 442376 | tf_op jit(solution)/shard_map/ppermute | solution.py:309
  102.0 5.9 %collective-permute-done.4.refs_2_ = bf16[4,144,128]{2,1,0:T(8,128)(2,1)S(1)} collective-permute-done((bf16[4,144,128]{2,1,0:T(8,128)(2,1)}, bf16[4,144,128]{2,1,0:T(8,128)(2,1)S(1)}, u32[]{:S(2)}, u32[]{:S(2)}) %collective-permute-start.4) | collective-permute-done | bytes 147488 | tf_op jit(solution)/shard_map/ppermute | solution.py:309
  108.0 0.3 collective-permute-start.9
  108.2 0.7 reshape.18
  108.9 0.0 all-to-all-done.parts_ref
  108.9 1.6 %first.1 = (bf16[2,200,4096]{2,1,0:T(8,128)(2,1)}, f32[2,128,128]{2,1,0:T(8,128)S(1)}) custom-call(bf16[32,2,128,128]{3,2,1,0:T(8,128)(2,1)S(1)} %all-to-all-done.parts_ref), custom_call_target="tpu_custom_call" | custom-call | tf_op jit(solution)/shard_map/first/pallas_call | solution.py:192
  110.5 5.8 %collective-permute-done.5.refs_3_ = bf16[4,144,128]{2,1,0:T(8,128)(2,1)S(1)} collective-permute-done((bf16[4,144,128]{2,1,0:T(8,128)(2,1)}, bf16[4,144,128]{2,1,0:T(8,128)(2,1)S(1)}, u32[]{:S(2)}, u32[]{:S(2)}) %collective-permute-start.5) | collective-permute-done | bytes 147488 | tf_op jit(solution)/shard_map/ppermute | solution.py:309
  116.3 4.6 %collective-permute-done.6.refs_4_ = bf16[4,144,128]{2,1,0:T(8,128)(2,1)S(1)} collective-permute-done((bf16[4,144,128]{2,1,0:T(8,128)(2,1)}, bf16[4,144,128]{2,1,0:T(8,128)(2,1)S(1)}, u32[]{:S(2)}, u32[]{:S(2)}) %collective-permute-start.6) | collective-permute-done | bytes 147488 | tf_op jit(solution)/shard_map/ppermute | solution.py:309
  120.9 0.0 collective-permute-done.7.refs_5_
  120.9 0.0 collective-permute-done.8.refs_6_
  120.9 0.0 collective-permute-done.9.refs_7_
  121.0 1.3 %last.1 = (bf16[2,200,4096]{2,1,0:T(8,128)(2,1)}, f32[2,200]{1,0:T(2,128)}) custom-call(f32[2,128,128]{2,1,0:T(8,128)S(1)} %get-tuple-element.19.first_ref, bf16[4,144,128]{2,1,0:T(8,128)(2,1)S(1)} %get-tuple-element.24.refs_0_, bf16[4,144,128]{2,1,0:T(8,128)(2,1)S(1)} %collective-permute-done.3.refs_1_, ...), custom_call_target="tpu_custom_call", output_to_operand_aliasing={{0}: (9, {})} | custom-call | tf_op jit(solution)/shard_map/last/pallas_call | solution.py:283
  (2 shorter events, 0.0 us)
Async XLA Ops:
  1.3 3.6 %collective-permute-start.10 = (bf16[2,128]{1,0:T(2,128)(2,1)S(1)}, bf16[2,128]{1,0:T(2,128)(2,1)S(1)}, u32[]{:S(2)}, u32[]{:S(2)}) collective-permute-start(bf16[2,128]{1,0:T(2,128)(2,1)S(1)} %fusion), channel_id=1, source_target_pairs={{0,1},{1,2},{2,3},{3,0},{4,5},{5,6},{6,7},{7,4},{8,9},{9,10},{10,1... | collective-permute-start | bytes 1544 | tf_op jit(solution)/shard_map/ppermute | solution.py:309
  3.5 5.1 %collective-permute-start.11 = (bf16[2,128]{1,0:T(2,128)(2,1)S(1)}, bf16[2,128]{1,0:T(2,128)(2,1)S(1)}, u32[]{:S(2)}, u32[]{:S(2)}) collective-permute-start(bf16[2,128]{1,0:T(2,128)(2,1)S(1)} %fusion), channel_id=1, source_target_pairs={{0,2},{1,3},{2,0},{3,1},{4,6},{5,7},{6,4},{7,5},{8,10},{9,11},{10,... | collective-permute-start | bytes 1544 | tf_op jit(solution)/shard_map/ppermute | solution.py:309
  4.2 4.8 %collective-permute-start.12 = (bf16[2,128]{1,0:T(2,128)(2,1)S(1)}, bf16[2,128]{1,0:T(2,128)(2,1)S(1)}, u32[]{:S(2)}, u32[]{:S(2)}) collective-permute-start(bf16[2,128]{1,0:T(2,128)(2,1)S(1)} %fusion), channel_id=1, source_target_pairs={{0,3},{1,0},{2,1},{3,2},{4,7},{5,4},{6,5},{7,6},{8,11},{9,8},{10,9... | collective-permute-start | bytes 1544 | tf_op jit(solution)/shard_map/ppermute | solution.py:309
  9.0 14.8 %collective-permute-start.13 = (bf16[8,128]{1,0:T(8,128)(2,1)S(1)}, bf16[8,128]{1,0:T(8,128)(2,1)S(1)}, u32[]{:S(2)}, u32[]{:S(2)}) collective-permute-start(bf16[8,128]{1,0:T(8,128)(2,1)S(1)} %pad_maximum_fusion.refs_0_), channel_id=1, source_target_pairs={{0,4},{1,5},{2,6},{3,7},{4,8},{5,9},{6,10},{7,11},{8,12},{9,13},{1... | collective-permute-start | bytes 6152 | tf_op jit(solution)/shard_map/ppermute | solution.py:309
  11.0 15.5 %collective-permute-start.14 = (bf16[8,128]{1,0:T(8,128)(2,1)S(1)}, bf16[8,128]{1,0:T(8,128)(2,1)S(1)}, u32[]{:S(2)}, u32[]{:S(2)}) collective-permute-start(bf16[8,128]{1,0:T(8,128)(2,1)S(1)} %pad_maximum_fusion.refs_0_), channel_id=1, source_target_pairs={{0,8},{1,9},{2,10},{3,11},{4,12},{5,13},{6,14},{7,15},{8,16},{9,17... | collective-permute-start | bytes 6152 | tf_op jit(solution)/shard_map/ppermute | solution.py:309
  14.3 13.2 %collective-permute-start.15 = (bf16[8,128]{1,0:T(8,128)(2,1)S(1)}, bf16[8,128]{1,0:T(8,128)(2,1)S(1)}, u32[]{:S(2)}, u32[]{:S(2)}) collective-permute-start(bf16[8,128]{1,0:T(8,128)(2,1)S(1)} %pad_maximum_fusion.refs_0_), channel_id=1, source_target_pairs={{0,12},{1,13},{2,14},{3,15},{4,16},{5,17},{6,18},{7,19},{8,20},{9,... | collective-permute-start | bytes 6152 | tf_op jit(solution)/shard_map/ppermute | solution.py:309
  18.3 9.2 %collective-permute-start.16 = (bf16[8,128]{1,0:T(8,128)(2,1)S(1)}, bf16[8,128]{1,0:T(8,128)(2,1)S(1)}, u32[]{:S(2)}, u32[]{:S(2)}) collective-permute-start(bf16[8,128]{1,0:T(8,128)(2,1)S(1)} %pad_maximum_fusion.refs_0_), channel_id=1, source_target_pairs={{0,16},{1,17},{2,18},{3,19},{4,20},{5,21},{6,22},{7,23},{8,24},{9,... | collective-permute-start | bytes 6152 | tf_op jit(solution)/shard_map/ppermute | solution.py:309
  18.9 8.6 %collective-permute-start.17 = (bf16[8,128]{1,0:T(8,128)(2,1)S(1)}, bf16[8,128]{1,0:T(8,128)(2,1)S(1)}, u32[]{:S(2)}, u32[]{:S(2)}) collective-permute-start(bf16[8,128]{1,0:T(8,128)(2,1)S(1)} %pad_maximum_fusion.refs_0_), channel_id=1, source_target_pairs={{0,20},{1,21},{2,22},{3,23},{4,24},{5,25},{6,26},{7,27},{8,28},{9,... | collective-permute-start | bytes 6152 | tf_op jit(solution)/shard_map/ppermute | solution.py:309
  23.8 4.5 %collective-permute-start.18 = (bf16[8,128]{1,0:T(8,128)(2,1)S(1)}, bf16[8,128]{1,0:T(8,128)(2,1)S(1)}, u32[]{:S(2)}, u32[]{:S(2)}) collective-permute-start(bf16[8,128]{1,0:T(8,128)(2,1)S(1)} %pad_maximum_fusion.refs_0_), channel_id=1, source_target_pairs={{0,24},{1,25},{2,26},{3,27},{4,28},{5,29},{6,30},{7,31},{8,0},{9,1... | collective-permute-start | bytes 6152 | tf_op jit(solution)/shard_map/ppermute | solution.py:309
  26.5 3.6 %collective-permute-start.19 = (bf16[8,128]{1,0:T(8,128)(2,1)S(1)}, bf16[8,128]{1,0:T(8,128)(2,1)S(1)}, u32[]{:S(2)}, u32[]{:S(2)}) collective-permute-start(bf16[8,128]{1,0:T(8,128)(2,1)S(1)} %pad_maximum_fusion.refs_0_), channel_id=1, source_target_pairs={{0,28},{1,29},{2,30},{3,31},{4,0},{5,1},{6,2},{7,3},{8,4},{9,5},{1... | collective-permute-start | bytes 6152 | tf_op jit(solution)/shard_map/ppermute | solution.py:309
  30.8 10.6 %all-to-all-start.1 = ((bf16[8,2,4096]{2,1,0:T(2,128)(2,1)}), bf16[8,2,4096]{2,1,0:T(2,128)(2,1)S(1)}, u32[]{:S(2)}, u32[]{:S(2)}) async-start(bf16[8,2,4096]{2,1,0:T(2,128)(2,1)} %router.1), calls=%async_computation.1 | async-start | bytes 262144 | tf_op jit(solution)/shard_map/all_to_all | solution.py:339
  41.4 67.5 %all-to-all-start = ((bf16[32,2,128,128]{3,2,1,0:T(8,128)(2,1)}), bf16[32,2,128,128]{3,2,1,0:T(8,128)(2,1)S(1)}, u32[]{:S(2)}, u32[]{:S(2)}) async-start(bf16[32,2,128,128]{3,2,1,0:T(8,128)(2,1)} %packed.1), calls=%async_computation | async-start | bytes 4194304 | tf_op jit(solution)/shard_map/all_to_all | solution.py:324
  51.7 22.5 %collective-permute-start = (bf16[8,144,128]{2,1,0:T(8,128)(2,1)}, bf16[8,144,128]{2,1,0:T(8,128)(2,1)S(1)}, u32[]{:S(2)}, u32[]{:S(2)}) collective-permute-start(bf16[8,144,128]{2,1,0:T(8,128)(2,1)} %get-tuple-element.21), channel_id=1, source_target_pairs={{0,1},{1,2},{2,3},{3,0},{4,5},{5,6},{6,7},{7,4},{8,9},{9,10},{10,1... | collective-permute-start | bytes 884744 | tf_op jit(solution)/shard_map/ppermute | solution.py:309
  52.0 22.2 %collective-permute-start.1 = (bf16[8,144,128]{2,1,0:T(8,128)(2,1)}, bf16[8,144,128]{2,1,0:T(8,128)(2,1)S(1)}, u32[]{:S(2)}, u32[]{:S(2)}) collective-permute-start(bf16[8,144,128]{2,1,0:T(8,128)(2,1)} %get-tuple-element.22), channel_id=1, source_target_pairs={{0,2},{1,3},{2,0},{3,1},{4,6},{5,7},{6,4},{7,5},{8,10},{9,11},{10,... | collective-permute-start | bytes 884744 | tf_op jit(solution)/shard_map/ppermute | solution.py:309
  54.7 27.9 %collective-permute-start.2 = (bf16[8,144,128]{2,1,0:T(8,128)(2,1)}, bf16[8,144,128]{2,1,0:T(8,128)(2,1)S(1)}, u32[]{:S(2)}, u32[]{:S(2)}) collective-permute-start(bf16[8,144,128]{2,1,0:T(8,128)(2,1)} %get-tuple-element.23), channel_id=1, source_target_pairs={{0,3},{1,0},{2,1},{3,2},{4,7},{5,4},{6,5},{7,6},{8,11},{9,8},{10,9... | collective-permute-start | bytes 884744 | tf_op jit(solution)/shard_map/ppermute | solution.py:309
  82.7 1.0 copy-start
  84.9 15.3 %collective-permute-start.3 = (bf16[4,144,128]{2,1,0:T(8,128)(2,1)}, bf16[4,144,128]{2,1,0:T(8,128)(2,1)S(1)}, u32[]{:S(2)}, u32[]{:S(2)}) collective-permute-start(bf16[4,144,128]{2,1,0:T(8,128)(2,1)} %get-tuple-element.25), channel_id=1, source_target_pairs={{0,4},{1,5},{2,6},{3,7},{4,8},{5,9},{6,10},{7,11},{8,12},{9,13},{1... | collective-permute-start | bytes 442376 | tf_op jit(solution)/shard_map/ppermute | solution.py:309
  85.0 23.0 %collective-permute-start.4 = (bf16[4,144,128]{2,1,0:T(8,128)(2,1)}, bf16[4,144,128]{2,1,0:T(8,128)(2,1)S(1)}, u32[]{:S(2)}, u32[]{:S(2)}) collective-permute-start(bf16[4,144,128]{2,1,0:T(8,128)(2,1)} %get-tuple-element.26), channel_id=1, source_target_pairs={{0,8},{1,9},{2,10},{3,11},{4,12},{5,13},{6,14},{7,15},{8,16},{9,17... | collective-permute-start | bytes 442376 | tf_op jit(solution)/shard_map/ppermute | solution.py:309
  86.0 30.3 %collective-permute-start.5 = (bf16[4,144,128]{2,1,0:T(8,128)(2,1)}, bf16[4,144,128]{2,1,0:T(8,128)(2,1)S(1)}, u32[]{:S(2)}, u32[]{:S(2)}) collective-permute-start(bf16[4,144,128]{2,1,0:T(8,128)(2,1)} %get-tuple-element.27), channel_id=1, source_target_pairs={{0,12},{1,13},{2,14},{3,15},{4,16},{5,17},{6,18},{7,19},{8,20},{9,... | collective-permute-start | bytes 442376 | tf_op jit(solution)/shard_map/ppermute | solution.py:309
  90.2 30.7 %collective-permute-start.6 = (bf16[4,144,128]{2,1,0:T(8,128)(2,1)}, bf16[4,144,128]{2,1,0:T(8,128)(2,1)S(1)}, u32[]{:S(2)}, u32[]{:S(2)}) collective-permute-start(bf16[4,144,128]{2,1,0:T(8,128)(2,1)} %get-tuple-element.28), channel_id=1, source_target_pairs={{0,16},{1,17},{2,18},{3,19},{4,20},{5,21},{6,22},{7,23},{8,24},{9,... | collective-permute-start | bytes 442376 | tf_op jit(solution)/shard_map/ppermute | solution.py:309
  91.7 29.2 %collective-permute-start.7 = (bf16[4,144,128]{2,1,0:T(8,128)(2,1)}, bf16[4,144,128]{2,1,0:T(8,128)(2,1)S(1)}, u32[]{:S(2)}, u32[]{:S(2)}) collective-permute-start(bf16[4,144,128]{2,1,0:T(8,128)(2,1)} %get-tuple-element.29), channel_id=1, source_target_pairs={{0,20},{1,21},{2,22},{3,23},{4,24},{5,25},{6,26},{7,27},{8,28},{9,... | collective-permute-start | bytes 442376 | tf_op jit(solution)/shard_map/ppermute | solution.py:309
  100.2 20.7 %collective-permute-start.8 = (bf16[4,144,128]{2,1,0:T(8,128)(2,1)}, bf16[4,144,128]{2,1,0:T(8,128)(2,1)S(1)}, u32[]{:S(2)}, u32[]{:S(2)}) collective-permute-start(bf16[4,144,128]{2,1,0:T(8,128)(2,1)} %get-tuple-element.30), channel_id=1, source_target_pairs={{0,24},{1,25},{2,26},{3,27},{4,28},{5,29},{6,30},{7,31},{8,0},{9,1... | collective-permute-start | bytes 442376 | tf_op jit(solution)/shard_map/ppermute | solution.py:309
  108.0 13.0 %collective-permute-start.9 = (bf16[4,144,128]{2,1,0:T(8,128)(2,1)}, bf16[4,144,128]{2,1,0:T(8,128)(2,1)S(1)}, u32[]{:S(2)}, u32[]{:S(2)}) collective-permute-start(bf16[4,144,128]{2,1,0:T(8,128)(2,1)} %get-tuple-element.31), channel_id=1, source_target_pairs={{0,28},{1,29},{2,30},{3,31},{4,0},{5,1},{6,2},{7,3},{8,4},{9,5},{1... | collective-permute-start | bytes 442376 | tf_op jit(solution)/shard_map/ppermute | solution.py:309

commit v2 on v1

--- a/solution.py
+++ b/solution.py
@@ -7,6 +7,7 @@
 
 
 RING, CROSS = 8, 4
+LAST_CUT = 40
 FIRST_ROWS = 128
 PACK_GROUPS = (16, 8, 4, 4)
 NORM_ROWS = 32
@@ -250,30 +251,36 @@
     out_ref, scale_ref, out_vmem, total_vmem, scale_vmem, sems, scale_sem = refs[RING + 1:]
     experts, rows, _ = out_vmem.shape
     first, lanes = first_ref.shape[1:]
+    cuts = ((0, LAST_CUT), (LAST_CUT, rows - LAST_CUT))
 
     def column(j, i):
         return column_at(j, i, lanes)
 
-    def copy(expert):
-        return pltpu.make_async_copy(out_vmem.at[expert], out_ref.at[expert, pl.ds(first, rows)], sems.at[expert])
+    def copy(expert, k):
+        start, size = cuts[k]
+        return pltpu.make_async_copy(
+            out_vmem.at[expert, pl.ds(start, size)], out_ref.at[expert, pl.ds(first + start, size)], sems.at[expert, k]
+        )
 
     scale_copy = pltpu.make_async_copy(scale_vmem, scale_ref, scale_sem)
     for expert in range(experts):
-        at = pl.ds(expert * rows, rows)
-        total = row_total([lambda j=j, i=i: parts[j][i, at] for j in range(RING) for i in range(CROSS)])
         total_vmem[expert, pl.ds(0, first)] = first_ref[expert]
-        total_vmem[expert, pl.ds(first, rows)] = total
-        inverse = inverse_scale(total)
-        for j in range(RING):
-            for i in range(CROSS):
-                part = parts[j][i, at].astype(jnp.float32)
-                out_vmem[expert, :, column(j, i)] = (part * inverse).astype(jnp.bfloat16)
-        copy(expert).start()
+        for k, (start, size) in enumerate(cuts):
+            at = pl.ds(expert * rows + start, size)
+            total = row_total([lambda j=j, i=i: parts[j][i, at] for j in range(RING) for i in range(CROSS)])
+            total_vmem[expert, pl.ds(first + start, size)] = total
+            inverse = inverse_scale(total)
+            for j in range(RING):
+                for i in range(CROSS):
+                    part = parts[j][i, at].astype(jnp.float32)
+                    out_vmem[expert, pl.ds(start, size), column(j, i)] = (part * inverse).astype(jnp.bfloat16)
+            copy(expert, k).start()
     for expert in range(experts):
         scale_vmem[pl.ds(expert, 1)] = jnp.sqrt(jnp.sum(jnp.transpose(total_vmem[expert]), axis=0, keepdims=True))
     scale_copy.start()
     for expert in range(experts):
-        copy(expert).wait()
+        for k in range(len(cuts)):
+            copy(expert, k).wait()
     scale_copy.wait()
 
 
@@ -293,7 +300,7 @@
             pltpu.VMEM((experts, rows, width), jnp.bfloat16),
             pltpu.VMEM((experts, full_rows, lanes), jnp.float32),
             pltpu.VMEM((experts, full_rows), jnp.float32),
-            pltpu.SemaphoreType.DMA((experts,)),
+            pltpu.SemaphoreType.DMA((experts, 2)),
             pltpu.SemaphoreType.DMA,
         ],
         input_output_aliases={1 + RING: 0},

time: 123 us -> 123 us (level)
  no operation moved by 1% of the time
where the time goes in v2:
time: 123 us; the launch traced here: 122 us
  waiting for transfers between devices  59.2 us (48%)
  starting transfers between devices  47.5 us (39%)
  Pallas kernels  12.4 us (10%)
  local copies, waits for them, and re-layouts  1.67 us (1%)
    ppermute x20, waiting for transfers between devices, moved(): return lax.ppermute(x, 'shard', pairs)  56.7 us
    ppermute x20, starting transfers between devices, moved(): return lax.ppermute(x, 'shard', pairs)  36.7 us
    all_to_all x1, starting transfers between devices, body(): received = lax.all_to_all(sent, 'shard', 0, 0, tiled=True)  6.32 us
    all_to_all x1, starting transfers between devices, body(): gathered = lax.all_to_all(copies, 'expert', 0, 0, tiled=True)  4.48 us
    pallas_call x1, Pallas kernels, sorted_by_cross(): pl.pallas_call(sorted_kernel, in_specs=[pl.BlockSpec(memory_space=pltpu.S...  3.95 us
    pallas_call x1, Pallas kernels, packed(): pl.pallas_call(packed_kernel, in_specs=[pl.BlockSpec(memory_space=pltpu.H...  3.61 us
    all_to_all x1, waiting for transfers between devices, body(): gathered = lax.all_to_all(copies, 'expert', 0, 0, tiled=True)  2.48 us
  transfers between devices with their start and end apart: 22, of which 12 were waited for; matrix products, arithmetic and copies ran while one was open for 1% of the time, Pallas kernels for 8%

profile of v2, /device:TPU:6, one launch (start us, length us, event | category | flops | bytes accessed | tf_op | source)
XLA Modules:
  0.0 122.4 jit_solution(2197660053040325379)
XLA Ops:
  0.6 0.7 fusion
  1.3 2.2 %collective-permute-start.10 = (bf16[2,128]{1,0:T(2,128)(2,1)S(1)}, bf16[2,128]{1,0:T(2,128)(2,1)S(1)}, u32[]{:S(2)}, u32[]{:S(2)}) collective-permute-start(bf16[2,128]{1,0:T(2,128)(2,1)S(1)} %fusion), channel_id=1, source_target_pairs={{0,1},{1,2},{2,3},{3,0},{4,5},{5,6},{6,7},{7,4},{8,9},{9,10},{10,1... | collective-permute-start | bytes 1544 | tf_op jit(solution)/shard_map/ppermute | solution.py:316
  3.5 0.7 collective-permute-start.11
  4.2 0.1 collective-permute-start.12
  4.4 0.5 collective-permute-done.10
  4.9 3.7 %collective-permute-done.11 = bf16[2,128]{1,0:T(2,128)(2,1)S(1)} collective-permute-done((bf16[2,128]{1,0:T(2,128)(2,1)S(1)}, bf16[2,128]{1,0:T(2,128)(2,1)S(1)}, u32[]{:S(2)}, u32[]{:S(2)}) %collective-permute-start.11) | collective-permute-done | bytes 544 | tf_op jit(solution)/shard_map/ppermute | solution.py:316
  8.6 0.4 collective-permute-done.12
  9.0 2.0 %collective-permute-start.13 = (bf16[8,128]{1,0:T(8,128)(2,1)S(1)}, bf16[8,128]{1,0:T(8,128)(2,1)S(1)}, u32[]{:S(2)}, u32[]{:S(2)}) collective-permute-start(bf16[8,128]{1,0:T(8,128)(2,1)S(1)} %pad_maximum_fusion.refs_0_), channel_id=1, source_target_pairs={{0,4},{1,5},{2,6},{3,7},{4,8},{5,9},{6,10},{7,11},{8,12},{9,13},{1... | collective-permute-start | bytes 6152 | tf_op jit(solution)/shard_map/ppermute | solution.py:316
  11.0 3.3 %collective-permute-start.14 = (bf16[8,128]{1,0:T(8,128)(2,1)S(1)}, bf16[8,128]{1,0:T(8,128)(2,1)S(1)}, u32[]{:S(2)}, u32[]{:S(2)}) collective-permute-start(bf16[8,128]{1,0:T(8,128)(2,1)S(1)} %pad_maximum_fusion.refs_0_), channel_id=1, source_target_pairs={{0,8},{1,9},{2,10},{3,11},{4,12},{5,13},{6,14},{7,15},{8,16},{9,17... | collective-permute-start | bytes 6152 | tf_op jit(solution)/shard_map/ppermute | solution.py:316
  14.3 4.0 %collective-permute-start.15 = (bf16[8,128]{1,0:T(8,128)(2,1)S(1)}, bf16[8,128]{1,0:T(8,128)(2,1)S(1)}, u32[]{:S(2)}, u32[]{:S(2)}) collective-permute-start(bf16[8,128]{1,0:T(8,128)(2,1)S(1)} %pad_maximum_fusion.refs_0_), channel_id=1, source_target_pairs={{0,12},{1,13},{2,14},{3,15},{4,16},{5,17},{6,18},{7,19},{8,20},{9,... | collective-permute-start | bytes 6152 | tf_op jit(solution)/shard_map/ppermute | solution.py:316
  18.3 0.5 collective-permute-start.16
  18.9 4.9 %collective-permute-start.17 = (bf16[8,128]{1,0:T(8,128)(2,1)S(1)}, bf16[8,128]{1,0:T(8,128)(2,1)S(1)}, u32[]{:S(2)}, u32[]{:S(2)}) collective-permute-start(bf16[8,128]{1,0:T(8,128)(2,1)S(1)} %pad_maximum_fusion.refs_0_), channel_id=1, source_target_pairs={{0,20},{1,21},{2,22},{3,23},{4,24},{5,25},{6,26},{7,27},{8,28},{9,... | collective-permute-start | bytes 6152 | tf_op jit(solution)/shard_map/ppermute | solution.py:316
  23.8 0.0 collective-permute-done.13.refs_1_
  23.8 2.7 %collective-permute-start.18 = (bf16[8,128]{1,0:T(8,128)(2,1)S(1)}, bf16[8,128]{1,0:T(8,128)(2,1)S(1)}, u32[]{:S(2)}, u32[]{:S(2)}) collective-permute-start(bf16[8,128]{1,0:T(8,128)(2,1)S(1)} %pad_maximum_fusion.refs_0_), channel_id=1, source_target_pairs={{0,24},{1,25},{2,26},{3,27},{4,28},{5,29},{6,30},{7,31},{8,0},{9,1... | collective-permute-start | bytes 6152 | tf_op jit(solution)/shard_map/ppermute | solution.py:316
  26.5 0.0 collective-permute-done.14.refs_2_
  26.5 1.0 collective-permute-start.19
  27.5 0.0 collective-permute-done.15.refs_3_
  27.5 0.0 collective-permute-done.16.refs_4_
  27.5 0.0 collective-permute-done.17.refs_5_
  27.5 0.8 collective-permute-done.18.refs_6_
  28.3 1.8 %collective-permute-done.19.refs_7_ = bf16[8,128]{1,0:T(8,128)(2,1)S(1)} collective-permute-done((bf16[8,128]{1,0:T(8,128)(2,1)S(1)}, bf16[8,128]{1,0:T(8,128)(2,1)S(1)}, u32[]{:S(2)}, u32[]{:S(2)}) %collective-permute-start.19) | collective-permute-done | bytes 2080 | tf_op jit(solution)/shard_map/ppermute | solution.py:316
  30.1 0.8 router.1
  30.8 4.5 %all-to-all-start.1 = ((bf16[8,2,4096]{2,1,0:T(2,128)(2,1)}), bf16[8,2,4096]{2,1,0:T(2,128)(2,1)S(1)}, u32[]{:S(2)}, u32[]{:S(2)}) async-start(bf16[8,2,4096]{2,1,0:T(2,128)(2,1)} %router.1), calls=%async_computation.1 | async-start | bytes 262144 | tf_op jit(solution)/shard_map/all_to_all | solution.py:346
  35.3 3.6 %packed.1 = bf16[32,2,128,128]{3,2,1,0:T(8,128)(2,1)} custom-call(f32[2,32,200,128]{3,2,1,0:T(8,128)} %bitcast.5, bf16[2,32,200,128]{3,2,1,0:T(8,128)(2,1)} %bitcast.7), custom_call_target="tpu_custom_call" | custom-call | tf_op jit(solution)/shard_map/packed/pallas_call | solution.py:55
  38.9 2.5 %all-to-all-done.1 = bf16[8,2,4096]{2,1,0:T(2,128)(2,1)S(1)} async-done(((bf16[8,2,4096]{2,1,0:T(2,128)(2,1)}), bf16[8,2,4096]{2,1,0:T(2,128)(2,1)S(1)}, u32[]{:S(2)}, u32[]{:S(2)}) %all-to-all-start.1) | async-done | bytes 131104 | tf_op jit(solution)/shard_map/all_to_all | solution.py:346
  41.4 6.3 %all-to-all-start = ((bf16[32,2,128,128]{3,2,1,0:T(8,128)(2,1)}), bf16[32,2,128,128]{3,2,1,0:T(8,128)(2,1)S(1)}, u32[]{:S(2)}, u32[]{:S(2)}) async-start(bf16[32,2,128,128]{3,2,1,0:T(8,128)(2,1)} %packed.1), calls=%async_computation | async-start | bytes 4194304 | tf_op jit(solution)/shard_map/all_to_all | solution.py:331
  47.8 4.0 %sorted.1 = (bf16[8,144,128]{2,1,0:T(8,128)(2,1)}, bf16[8,144,128]{2,1,0:T(8,128)(2,1)}, bf16[8,144,128]{2,1,0:T(8,128)(2,1)}, bf16[8,144,128]{2,1,0:T(8,128)(2,1)}) custom-call(s32[32]{0:T(128)S(1)} %and_or_fusion.targets, f32[2,32,200,128]{3,2,1,0:T(8,128)} %bitcast.6, bf16[2,32,200,128]{3,2,1,0:T(8,128)(2,1)} %bitcast.8), custom_call_target="tpu_custom_call" | custom-call | tf_op jit(solution)/shard_map/sorted/pallas_call | solution.py:108
  51.7 0.3 collective-permute-start
  52.0 2.7 %collective-permute-start.1 = (bf16[8,144,128]{2,1,0:T(8,128)(2,1)}, bf16[8,144,128]{2,1,0:T(8,128)(2,1)S(1)}, u32[]{:S(2)}, u32[]{:S(2)}) collective-permute-start(bf16[8,144,128]{2,1,0:T(8,128)(2,1)} %get-tuple-element.22), channel_id=1, source_target_pairs={{0,2},{1,3},{2,0},{3,1},{4,6},{5,7},{6,4},{7,5},{8,10},{9,11},{10,... | collective-permute-start | bytes 884744 | tf_op jit(solution)/shard_map/ppermute | solution.py:316
  54.7 0.0 collective-permute-start.2
  54.7 19.5 %collective-permute-done.refs_1_ = bf16[8,144,128]{2,1,0:T(8,128)(2,1)S(1)} collective-permute-done((bf16[8,144,128]{2,1,0:T(8,128)(2,1)}, bf16[8,144,128]{2,1,0:T(8,128)(2,1)S(1)}, u32[]{:S(2)}, u32[]{:S(2)}) %collective-permute-start) | collective-permute-done | bytes 294944 | tf_op jit(solution)/shard_map/ppermute | solution.py:316
  74.3 0.0 collective-permute-done.1.refs_2_
  74.3 8.4 %collective-permute-done.2.refs_3_ = bf16[8,144,128]{2,1,0:T(8,128)(2,1)S(1)} collective-permute-done((bf16[8,144,128]{2,1,0:T(8,128)(2,1)}, bf16[8,144,128]{2,1,0:T(8,128)(2,1)S(1)}, u32[]{:S(2)}, u32[]{:S(2)}) %collective-permute-start.2) | collective-permute-done | bytes 294944 | tf_op jit(solution)/shard_map/ppermute | solution.py:316
  82.7 0.0 copy-start
  82.7 1.0 copy-done
  83.6 1.3 %turned.1 = (bf16[4,144,128]{2,1,0:T(8,128)(2,1)S(1)}, bf16[4,144,128]{2,1,0:T(8,128)(2,1)}, bf16[4,144,128]{2,1,0:T(8,128)(2,1)}, bf16[4,144,128]{2,1,0:T(8,128...) custom-call(bf16[8,144,128]{2,1,0:T(8,128)(2,1)S(1)} %copy-done, ...), custom_call_target="tpu_custom_call" | custom-call | tf_op jit(solution)/shard_map/turned/pallas_call | solution.py:144
  84.9 0.1 collective-permute-start.3
  85.0 1.0 collective-permute-start.4
  86.0 4.2 %collective-permute-start.5 = (bf16[4,144,128]{2,1,0:T(8,128)(2,1)}, bf16[4,144,128]{2,1,0:T(8,128)(2,1)S(1)}, u32[]{:S(2)}, u32[]{:S(2)}) collective-permute-start(bf16[4,144,128]{2,1,0:T(8,128)(2,1)} %get-tuple-element.27), channel_id=1, source_target_pairs={{0,12},{1,13},{2,14},{3,15},{4,16},{5,17},{6,18},{7,19},{8,20},{9,... | collective-permute-start | bytes 442376 | tf_op jit(solution)/shard_map/ppermute | solution.py:316
  90.2 1.5 %collective-permute-start.6 = (bf16[4,144,128]{2,1,0:T(8,128)(2,1)}, bf16[4,144,128]{2,1,0:T(8,128)(2,1)S(1)}, u32[]{:S(2)}, u32[]{:S(2)}) collective-permute-start(bf16[4,144,128]{2,1,0:T(8,128)(2,1)} %get-tuple-element.28), channel_id=1, source_target_pairs={{0,16},{1,17},{2,18},{3,19},{4,20},{5,21},{6,22},{7,23},{8,24},{9,... | collective-permute-start | bytes 442376 | tf_op jit(solution)/shard_map/ppermute | solution.py:316
  91.7 3.3 %collective-permute-start.7 = (bf16[4,144,128]{2,1,0:T(8,128)(2,1)}, bf16[4,144,128]{2,1,0:T(8,128)(2,1)S(1)}, u32[]{:S(2)}, u32[]{:S(2)}) collective-permute-start(bf16[4,144,128]{2,1,0:T(8,128)(2,1)} %get-tuple-element.29), channel_id=1, source_target_pairs={{0,20},{1,21},{2,22},{3,23},{4,24},{5,25},{6,26},{7,27},{8,28},{9,... | collective-permute-start | bytes 442376 | tf_op jit(solution)/shard_map/ppermute | solution.py:316
  95.0 5.2 %collective-permute-done.3.refs_1_ = bf16[4,144,128]{2,1,0:T(8,128)(2,1)S(1)} collective-permute-done((bf16[4,144,128]{2,1,0:T(8,128)(2,1)}, bf16[4,144,128]{2,1,0:T(8,128)(2,1)S(1)}, u32[]{:S(2)}, u32[]{:S(2)}) %collective-permute-start.3) | collective-permute-done | bytes 147488 | tf_op jit(solution)/shard_map/ppermute | solution.py:316
  100.2 1.8 %collective-permute-start.8 = (bf16[4,144,128]{2,1,0:T(8,128)(2,1)}, bf16[4,144,128]{2,1,0:T(8,128)(2,1)S(1)}, u32[]{:S(2)}, u32[]{:S(2)}) collective-permute-start(bf16[4,144,128]{2,1,0:T(8,128)(2,1)} %get-tuple-element.30), channel_id=1, source_target_pairs={{0,24},{1,25},{2,26},{3,27},{4,28},{5,29},{6,30},{7,31},{8,0},{9,1... | collective-permute-start | bytes 442376 | tf_op jit(solution)/shard_map/ppermute | solution.py:316
  102.0 5.9 %collective-permute-done.4.refs_2_ = bf16[4,144,128]{2,1,0:T(8,128)(2,1)S(1)} collective-permute-done((bf16[4,144,128]{2,1,0:T(8,128)(2,1)}, bf16[4,144,128]{2,1,0:T(8,128)(2,1)S(1)}, u32[]{:S(2)}, u32[]{:S(2)}) %collective-permute-start.4) | collective-permute-done | bytes 147488 | tf_op jit(solution)/shard_map/ppermute | solution.py:316
  108.0 0.3 collective-permute-start.9
  108.2 0.7 reshape.18
  108.9 0.0 all-to-all-done.parts_ref
  108.9 1.6 %first.1 = (bf16[2,200,4096]{2,1,0:T(8,128)(2,1)}, f32[2,128,128]{2,1,0:T(8,128)S(1)}) custom-call(bf16[32,2,128,128]{3,2,1,0:T(8,128)(2,1)S(1)} %all-to-all-done.parts_ref), custom_call_target="tpu_custom_call" | custom-call | tf_op jit(solution)/shard_map/first/pallas_call | solution.py:193
  110.5 5.8 %collective-permute-done.5.refs_3_ = bf16[4,144,128]{2,1,0:T(8,128)(2,1)S(1)} collective-permute-done((bf16[4,144,128]{2,1,0:T(8,128)(2,1)}, bf16[4,144,128]{2,1,0:T(8,128)(2,1)S(1)}, u32[]{:S(2)}, u32[]{:S(2)}) %collective-permute-start.5) | collective-permute-done | bytes 147488 | tf_op jit(solution)/shard_map/ppermute | solution.py:316
  116.3 4.6 %collective-permute-done.6.refs_4_ = bf16[4,144,128]{2,1,0:T(8,128)(2,1)S(1)} collective-permute-done((bf16[4,144,128]{2,1,0:T(8,128)(2,1)}, bf16[4,144,128]{2,1,0:T(8,128)(2,1)S(1)}, u32[]{:S(2)}, u32[]{:S(2)}) %collective-permute-start.6) | collective-permute-done | bytes 147488 | tf_op jit(solution)/shard_map/ppermute | solution.py:316
  120.9 0.0 collective-permute-done.7.refs_5_
  120.9 0.0 collective-permute-done.8.refs_6_
  120.9 0.0 collective-permute-done.9.refs_7_
  121.0 1.3 %last.1 = (bf16[2,200,4096]{2,1,0:T(8,128)(2,1)}, f32[2,200]{1,0:T(2,128)}) custom-call(f32[2,128,128]{2,1,0:T(8,128)S(1)} %get-tuple-element.19.first_ref, bf16[4,144,128]{2,1,0:T(8,128)(2,1)S(1)} %get-tuple-element.24.refs_0_, bf16[4,144,128]{2,1,0:T(8,128)(2,1)S(1)} %collective-permute-done.3.refs_1_, ...), custom_call_target="tpu_custom_call", output_to_operand_aliasing={{0}: (9, {})} | custom-call | tf_op jit(solution)/shard_map/last/pallas_call | solution.py:290
  (2 shorter events, 0.0 us)
Async XLA Ops:
  1.3 3.6 %collective-permute-start.10 = (bf16[2,128]{1,0:T(2,128)(2,1)S(1)}, bf16[2,128]{1,0:T(2,128)(2,1)S(1)}, u32[]{:S(2)}, u32[]{:S(2)}) collective-permute-start(bf16[2,128]{1,0:T(2,128)(2,1)S(1)} %fusion), channel_id=1, source_target_pairs={{0,1},{1,2},{2,3},{3,0},{4,5},{5,6},{6,7},{7,4},{8,9},{9,10},{10,1... | collective-permute-start | bytes 1544 | tf_op jit(solution)/shard_map/ppermute | solution.py:316
  3.5 5.1 %collective-permute-start.11 = (bf16[2,128]{1,0:T(2,128)(2,1)S(1)}, bf16[2,128]{1,0:T(2,128)(2,1)S(1)}, u32[]{:S(2)}, u32[]{:S(2)}) collective-permute-start(bf16[2,128]{1,0:T(2,128)(2,1)S(1)} %fusion), channel_id=1, source_target_pairs={{0,2},{1,3},{2,0},{3,1},{4,6},{5,7},{6,4},{7,5},{8,10},{9,11},{10,... | collective-permute-start | bytes 1544 | tf_op jit(solution)/shard_map/ppermute | solution.py:316
  4.2 4.8 %collective-permute-start.12 = (bf16[2,128]{1,0:T(2,128)(2,1)S(1)}, bf16[2,128]{1,0:T(2,128)(2,1)S(1)}, u32[]{:S(2)}, u32[]{:S(2)}) collective-permute-start(bf16[2,128]{1,0:T(2,128)(2,1)S(1)} %fusion), channel_id=1, source_target_pairs={{0,3},{1,0},{2,1},{3,2},{4,7},{5,4},{6,5},{7,6},{8,11},{9,8},{10,9... | collective-permute-start | bytes 1544 | tf_op jit(solution)/shard_map/ppermute | solution.py:316
  9.0 14.8 %collective-permute-start.13 = (bf16[8,128]{1,0:T(8,128)(2,1)S(1)}, bf16[8,128]{1,0:T(8,128)(2,1)S(1)}, u32[]{:S(2)}, u32[]{:S(2)}) collective-permute-start(bf16[8,128]{1,0:T(8,128)(2,1)S(1)} %pad_maximum_fusion.refs_0_), channel_id=1, source_target_pairs={{0,4},{1,5},{2,6},{3,7},{4,8},{5,9},{6,10},{7,11},{8,12},{9,13},{1... | collective-permute-start | bytes 6152 | tf_op jit(solution)/shard_map/ppermute | solution.py:316
  11.0 15.5 %collective-permute-start.14 = (bf16[8,128]{1,0:T(8,128)(2,1)S(1)}, bf16[8,128]{1,0:T(8,128)(2,1)S(1)}, u32[]{:S(2)}, u32[]{:S(2)}) collective-permute-start(bf16[8,128]{1,0:T(8,128)(2,1)S(1)} %pad_maximum_fusion.refs_0_), channel_id=1, source_target_pairs={{0,8},{1,9},{2,10},{3,11},{4,12},{5,13},{6,14},{7,15},{8,16},{9,17... | collective-permute-start | bytes 6152 | tf_op jit(solution)/shard_map/ppermute | solution.py:316
  14.3 13.2 %collective-permute-start.15 = (bf16[8,128]{1,0:T(8,128)(2,1)S(1)}, bf16[8,128]{1,0:T(8,128)(2,1)S(1)}, u32[]{:S(2)}, u32[]{:S(2)}) collective-permute-start(bf16[8,128]{1,0:T(8,128)(2,1)S(1)} %pad_maximum_fusion.refs_0_), channel_id=1, source_target_pairs={{0,12},{1,13},{2,14},{3,15},{4,16},{5,17},{6,18},{7,19},{8,20},{9,... | collective-permute-start | bytes 6152 | tf_op jit(solution)/shard_map/ppermute | solution.py:316
  18.3 9.2 %collective-permute-start.16 = (bf16[8,128]{1,0:T(8,128)(2,1)S(1)}, bf16[8,128]{1,0:T(8,128)(2,1)S(1)}, u32[]{:S(2)}, u32[]{:S(2)}) collective-permute-start(bf16[8,128]{1,0:T(8,128)(2,1)S(1)} %pad_maximum_fusion.refs_0_), channel_id=1, source_target_pairs={{0,16},{1,17},{2,18},{3,19},{4,20},{5,21},{6,22},{7,23},{8,24},{9,... | collective-permute-start | bytes 6152 | tf_op jit(solution)/shard_map/ppermute | solution.py:316
  18.9 8.6 %collective-permute-start.17 = (bf16[8,128]{1,0:T(8,128)(2,1)S(1)}, bf16[8,128]{1,0:T(8,128)(2,1)S(1)}, u32[]{:S(2)}, u32[]{:S(2)}) collective-permute-start(bf16[8,128]{1,0:T(8,128)(2,1)S(1)} %pad_maximum_fusion.refs_0_), channel_id=1, source_target_pairs={{0,20},{1,21},{2,22},{3,23},{4,24},{5,25},{6,26},{7,27},{8,28},{9,... | collective-permute-start | bytes 6152 | tf_op jit(solution)/shard_map/ppermute | solution.py:316
  23.8 4.5 %collective-permute-start.18 = (bf16[8,128]{1,0:T(8,128)(2,1)S(1)}, bf16[8,128]{1,0:T(8,128)(2,1)S(1)}, u32[]{:S(2)}, u32[]{:S(2)}) collective-permute-start(bf16[8,128]{1,0:T(8,128)(2,1)S(1)} %pad_maximum_fusion.refs_0_), channel_id=1, source_target_pairs={{0,24},{1,25},{2,26},{3,27},{4,28},{5,29},{6,30},{7,31},{8,0},{9,1... | collective-permute-start | bytes 6152 | tf_op jit(solution)/shard_map/ppermute | solution.py:316
  26.5 3.6 %collective-permute-start.19 = (bf16[8,128]{1,0:T(8,128)(2,1)S(1)}, bf16[8,128]{1,0:T(8,128)(2,1)S(1)}, u32[]{:S(2)}, u32[]{:S(2)}) collective-permute-start(bf16[8,128]{1,0:T(8,128)(2,1)S(1)} %pad_maximum_fusion.refs_0_), channel_id=1, source_target_pairs={{0,28},{1,29},{2,30},{3,31},{4,0},{5,1},{6,2},{7,3},{8,4},{9,5},{1... | collective-permute-start | bytes 6152 | tf_op jit(solution)/shard_map/ppermute | solution.py:316
  30.8 10.6 %all-to-all-start.1 = ((bf16[8,2,4096]{2,1,0:T(2,128)(2,1)}), bf16[8,2,4096]{2,1,0:T(2,128)(2,1)S(1)}, u32[]{:S(2)}, u32[]{:S(2)}) async-start(bf16[8,2,4096]{2,1,0:T(2,128)(2,1)} %router.1), calls=%async_computation.1 | async-start | bytes 262144 | tf_op jit(solution)/shard_map/all_to_all | solution.py:346
  41.4 67.5 %all-to-all-start = ((bf16[32,2,128,128]{3,2,1,0:T(8,128)(2,1)}), bf16[32,2,128,128]{3,2,1,0:T(8,128)(2,1)S(1)}, u32[]{:S(2)}, u32[]{:S(2)}) async-start(bf16[32,2,128,128]{3,2,1,0:T(8,128)(2,1)} %packed.1), calls=%async_computation | async-start | bytes 4194304 | tf_op jit(solution)/shard_map/all_to_all | solution.py:331
  51.7 22.5 %collective-permute-start = (bf16[8,144,128]{2,1,0:T(8,128)(2,1)}, bf16[8,144,128]{2,1,0:T(8,128)(2,1)S(1)}, u32[]{:S(2)}, u32[]{:S(2)}) collective-permute-start(bf16[8,144,128]{2,1,0:T(8,128)(2,1)} %get-tuple-element.21), channel_id=1, source_target_pairs={{0,1},{1,2},{2,3},{3,0},{4,5},{5,6},{6,7},{7,4},{8,9},{9,10},{10,1... | collective-permute-start | bytes 884744 | tf_op jit(solution)/shard_map/ppermute | solution.py:316
  52.0 22.2 %collective-permute-start.1 = (bf16[8,144,128]{2,1,0:T(8,128)(2,1)}, bf16[8,144,128]{2,1,0:T(8,128)(2,1)S(1)}, u32[]{:S(2)}, u32[]{:S(2)}) collective-permute-start(bf16[8,144,128]{2,1,0:T(8,128)(2,1)} %get-tuple-element.22), channel_id=1, source_target_pairs={{0,2},{1,3},{2,0},{3,1},{4,6},{5,7},{6,4},{7,5},{8,10},{9,11},{10,... | collective-permute-start | bytes 884744 | tf_op jit(solution)/shard_map/ppermute | solution.py:316
  54.7 27.9 %collective-permute-start.2 = (bf16[8,144,128]{2,1,0:T(8,128)(2,1)}, bf16[8,144,128]{2,1,0:T(8,128)(2,1)S(1)}, u32[]{:S(2)}, u32[]{:S(2)}) collective-permute-start(bf16[8,144,128]{2,1,0:T(8,128)(2,1)} %get-tuple-element.23), channel_id=1, source_target_pairs={{0,3},{1,0},{2,1},{3,2},{4,7},{5,4},{6,5},{7,6},{8,11},{9,8},{10,9... | collective-permute-start | bytes 884744 | tf_op jit(solution)/shard_map/ppermute | solution.py:316
  82.7 1.0 copy-start
  84.9 15.3 %collective-permute-start.3 = (bf16[4,144,128]{2,1,0:T(8,128)(2,1)}, bf16[4,144,128]{2,1,0:T(8,128)(2,1)S(1)}, u32[]{:S(2)}, u32[]{:S(2)}) collective-permute-start(bf16[4,144,128]{2,1,0:T(8,128)(2,1)} %get-tuple-element.25), channel_id=1, source_target_pairs={{0,4},{1,5},{2,6},{3,7},{4,8},{5,9},{6,10},{7,11},{8,12},{9,13},{1... | collective-permute-start | bytes 442376 | tf_op jit(solution)/shard_map/ppermute | solution.py:316
  85.0 23.0 %collective-permute-start.4 = (bf16[4,144,128]{2,1,0:T(8,128)(2,1)}, bf16[4,144,128]{2,1,0:T(8,128)(2,1)S(1)}, u32[]{:S(2)}, u32[]{:S(2)}) collective-permute-start(bf16[4,144,128]{2,1,0:T(8,128)(2,1)} %get-tuple-element.26), channel_id=1, source_target_pairs={{0,8},{1,9},{2,10},{3,11},{4,12},{5,13},{6,14},{7,15},{8,16},{9,17... | collective-permute-start | bytes 442376 | tf_op jit(solution)/shard_map/ppermute | solution.py:316
  86.0 30.3 %collective-permute-start.5 = (bf16[4,144,128]{2,1,0:T(8,128)(2,1)}, bf16[4,144,128]{2,1,0:T(8,128)(2,1)S(1)}, u32[]{:S(2)}, u32[]{:S(2)}) collective-permute-start(bf16[4,144,128]{2,1,0:T(8,128)(2,1)} %get-tuple-element.27), channel_id=1, source_target_pairs={{0,12},{1,13},{2,14},{3,15},{4,16},{5,17},{6,18},{7,19},{8,20},{9,... | collective-permute-start | bytes 442376 | tf_op jit(solution)/shard_map/ppermute | solution.py:316
  90.2 30.7 %collective-permute-start.6 = (bf16[4,144,128]{2,1,0:T(8,128)(2,1)}, bf16[4,144,128]{2,1,0:T(8,128)(2,1)S(1)}, u32[]{:S(2)}, u32[]{:S(2)}) collective-permute-start(bf16[4,144,128]{2,1,0:T(8,128)(2,1)} %get-tuple-element.28), channel_id=1, source_target_pairs={{0,16},{1,17},{2,18},{3,19},{4,20},{5,21},{6,22},{7,23},{8,24},{9,... | collective-permute-start | bytes 442376 | tf_op jit(solution)/shard_map/ppermute | solution.py:316
  91.7 29.2 %collective-permute-start.7 = (bf16[4,144,128]{2,1,0:T(8,128)(2,1)}, bf16[4,144,128]{2,1,0:T(8,128)(2,1)S(1)}, u32[]{:S(2)}, u32[]{:S(2)}) collective-permute-start(bf16[4,144,128]{2,1,0:T(8,128)(2,1)} %get-tuple-element.29), channel_id=1, source_target_pairs={{0,20},{1,21},{2,22},{3,23},{4,24},{5,25},{6,26},{7,27},{8,28},{9,... | collective-permute-start | bytes 442376 | tf_op jit(solution)/shard_map/ppermute | solution.py:316
  100.2 20.7 %collective-permute-start.8 = (bf16[4,144,128]{2,1,0:T(8,128)(2,1)}, bf16[4,144,128]{2,1,0:T(8,128)(2,1)S(1)}, u32[]{:S(2)}, u32[]{:S(2)}) collective-permute-start(bf16[4,144,128]{2,1,0:T(8,128)(2,1)} %get-tuple-element.30), channel_id=1, source_target_pairs={{0,24},{1,25},{2,26},{3,27},{4,28},{5,29},{6,30},{7,31},{8,0},{9,1... | collective-permute-start | bytes 442376 | tf_op jit(solution)/shard_map/ppermute | solution.py:316
  108.0 13.0 %collective-permute-start.9 = (bf16[4,144,128]{2,1,0:T(8,128)(2,1)}, bf16[4,144,128]{2,1,0:T(8,128)(2,1)S(1)}, u32[]{:S(2)}, u32[]{:S(2)}) collective-permute-start(bf16[4,144,128]{2,1,0:T(8,128)(2,1)} %get-tuple-element.31), channel_id=1, source_target_pairs={{0,28},{1,29},{2,30},{3,31},{4,0},{5,1},{6,2},{7,3},{8,4},{9,5},{1... | collective-permute-start | bytes 442376 | tf_op jit(solution)/shard_map/ppermute | solution.py:316

commit v3 on v2

--- a/solution.py
+++ b/solution.py
@@ -8,6 +8,7 @@
 
 RING, CROSS = 8, 4
 LAST_CUT = 40
+LATE = (1, 7)
 FIRST_ROWS = 128
 PACK_GROUPS = (16, 8, 4, 4)
 NORM_ROWS = 32
@@ -246,7 +247,28 @@
     )(*[pltpu.with_memory_space_constraint(tile, pltpu.VMEM) for tile in tiles])
 
 
-def last_kernel(first_ref, *refs):
+def middle_kernel(*refs):
+    parts, total_ref = refs[:-1], refs[-1]
+    experts, rows, _ = total_ref.shape
+    for expert in range(experts):
+        for start, size in ((0, LAST_CUT), (LAST_CUT, rows - LAST_CUT)):
+            at = pl.ds(expert * rows + start, size)
+            total_ref[expert, pl.ds(start, size)] = row_total([lambda p=p, i=i: p[i, at] for p in parts for i in range(CROSS)])
+
+
+def middle_totals(parts, experts):
+    rows, lanes = parts[0].shape[1] // experts, parts[0].shape[2]
+    return pl.pallas_call(
+        middle_kernel,
+        in_specs=[pl.BlockSpec(memory_space=pltpu.VMEM)] * len(parts),
+        out_specs=pl.BlockSpec(memory_space=pltpu.VMEM),
+        out_shape=pltpu.VMEM((experts, rows, lanes), jnp.float32),
+        compiler_params=pltpu.CompilerParams(vmem_limit_bytes=VMEM_LIMIT),
+        name="middle",
+    )(*[pltpu.with_memory_space_constraint(part, pltpu.VMEM) for part in parts])
+
+
+def last_kernel(first_ref, middle_ref, *refs):
     parts = refs[:RING]
     out_ref, scale_ref, out_vmem, total_vmem, scale_vmem, sems, scale_sem = refs[RING + 1:]
     experts, rows, _ = out_vmem.shape
@@ -267,7 +289,9 @@
         total_vmem[expert, pl.ds(0, first)] = first_ref[expert]
         for k, (start, size) in enumerate(cuts):
             at = pl.ds(expert * rows + start, size)
-            total = row_total([lambda j=j, i=i: parts[j][i, at] for j in range(RING) for i in range(CROSS)])
+            total = middle_ref[expert, pl.ds(start, size)] + row_total(
+                [lambda j=j, i=i: parts[j][i, at] for j in LATE for i in range(CROSS)]
+            )
             total_vmem[expert, pl.ds(first + start, size)] = total
             inverse = inverse_scale(total)
             for j in range(RING):
@@ -284,12 +308,12 @@
     scale_copy.wait()
 
 
-def last_normed(totals, parts, final):
+def last_normed(totals, middle, parts, final):
     experts, full_rows, width = final.shape
     rows, lanes = full_rows - totals.shape[1], totals.shape[2]
     return pl.pallas_call(
         last_kernel,
-        in_specs=[pl.BlockSpec(memory_space=pltpu.VMEM)] * (1 + RING)
+        in_specs=[pl.BlockSpec(memory_space=pltpu.VMEM)] * (2 + RING)
         + [pl.BlockSpec(memory_space=pltpu.HBM)],
         out_specs=[pl.BlockSpec(memory_space=pltpu.HBM)] * 2,
         out_shape=[
@@ -303,10 +327,10 @@
             pltpu.SemaphoreType.DMA((experts, 2)),
             pltpu.SemaphoreType.DMA,
         ],
-        input_output_aliases={1 + RING: 0},
+        input_output_aliases={2 + RING: 0},
         compiler_params=pltpu.CompilerParams(vmem_limit_bytes=VMEM_LIMIT),
         name="last",
-    )(*[pltpu.with_memory_space_constraint(x, pltpu.VMEM) for x in (totals, *parts)], final)
+    )(*[pltpu.with_memory_space_constraint(x, pltpu.VMEM) for x in (totals, middle, *parts)], final)
 
 
 def moved(x, dz, dx):
@@ -346,7 +370,8 @@
     gathered = lax.all_to_all(copies, "expert", 0, 0, tiled=True)
     final_down, totals = first_normed(received, rows)
     serve_router = gathered.reshape(-1, shards * lanes)
-    final_down, scale_down = last_normed(totals, blocks, final_down)
+    middle = middle_totals([blocks[j] for j in range(RING) if j not in LATE], experts)
+    final_down, scale_down = last_normed(totals, middle, blocks, final_down)
     return (final_down, scale_down, serve_router.T)
 
 

time: 123 us -> 126 us (1.024)
  starting transfers between devices: 47.5 us -> 51.7 us
    ppermute x20, starting transfers between devices: 36.7 us -> 40.9 us  [moved(): return lax.ppermute(x, 'shard', pairs)]
  transfers between devices with their start and end apart: 22 -> 22, of which waited for: 12 -> 11; matrix products, arithmetic and copies ran while one was open for 1% -> 1% of each run, Pallas kernels for 8% -> 8%
where the time goes in v3:
time: 126 us
  waiting for transfers between devices  58.5 us (46%)
  starting transfers between devices  51.7 us (41%)
  Pallas kernels  12.5 us (10%)
  local copies, waits for them, and re-layouts  1.67 us (1%)
    ppermute x20, waiting for transfers between devices, moved(): return lax.ppermute(x, 'shard', pairs)  56 us
    ppermute x20, starting transfers between devices, moved(): return lax.ppermute(x, 'shard', pairs)  40.9 us
    all_to_all x1, starting transfers between devices, body(): received = lax.all_to_all(sent, 'shard', 0, 0, tiled=True)  6.32 us
    all_to_all x1, starting transfers between devices, body(): gathered = lax.all_to_all(copies, 'expert', 0, 0, tiled=True)  4.48 us
    pallas_call x1, Pallas kernels, sorted_by_cross(): pl.pallas_call(sorted_kernel, in_specs=[pl.BlockSpec(memory_space=pltpu.S...  3.95 us
    pallas_call x1, Pallas kernels, packed(): pl.pallas_call(packed_kernel, in_specs=[pl.BlockSpec(memory_space=pltpu.H...  3.61 us
  transfers between devices with their start and end apart: 22, of which 11 were waited for; matrix products, arithmetic and copies ran while one was open for 1% of the time, Pallas kernels for 8%

profile of v3, /device:TPU:6, one launch (start us, length us, event | category | flops | bytes accessed | tf_op | source)
XLA Modules:
  0.0 125.9 jit_solution(5889532646401279169)
XLA Ops:
  0.6 0.7 fusion
  1.3 2.2 %collective-permute-start.10 = (bf16[2,128]{1,0:T(2,128)(2,1)S(1)}, bf16[2,128]{1,0:T(2,128)(2,1)S(1)}, u32[]{:S(2)}, u32[]{:S(2)}) collective-permute-start(bf16[2,128]{1,0:T(2,128)(2,1)S(1)} %fusion), channel_id=1, source_target_pairs={{0,1},{1,2},{2,3},{3,0},{4,5},{5,6},{6,7},{7,4},{8,9},{9,10},{10,1... | collective-permute-start | bytes 1544 | tf_op jit(solution)/shard_map/ppermute | solution.py:340
  3.5 0.7 collective-permute-start.11
  4.2 0.1 collective-permute-start.12
  4.4 0.5 collective-permute-done.10
  4.9 3.7 %collective-permute-done.11 = bf16[2,128]{1,0:T(2,128)(2,1)S(1)} collective-permute-done((bf16[2,128]{1,0:T(2,128)(2,1)S(1)}, bf16[2,128]{1,0:T(2,128)(2,1)S(1)}, u32[]{:S(2)}, u32[]{:S(2)}) %collective-permute-start.11) | collective-permute-done | bytes 544 | tf_op jit(solution)/shard_map/ppermute | solution.py:340
  8.6 0.4 collective-permute-done.12
  9.0 2.0 %collective-permute-start.13 = (bf16[8,128]{1,0:T(8,128)(2,1)S(1)}, bf16[8,128]{1,0:T(8,128)(2,1)S(1)}, u32[]{:S(2)}, u32[]{:S(2)}) collective-permute-start(bf16[8,128]{1,0:T(8,128)(2,1)S(1)} %pad_maximum_fusion.refs_0_), channel_id=1, source_target_pairs={{0,4},{1,5},{2,6},{3,7},{4,8},{5,9},{6,10},{7,11},{8,12},{9,13},{1... | collective-permute-start | bytes 6152 | tf_op jit(solution)/shard_map/ppermute | solution.py:340
  11.0 3.3 %collective-permute-start.14 = (bf16[8,128]{1,0:T(8,128)(2,1)S(1)}, bf16[8,128]{1,0:T(8,128)(2,1)S(1)}, u32[]{:S(2)}, u32[]{:S(2)}) collective-permute-start(bf16[8,128]{1,0:T(8,128)(2,1)S(1)} %pad_maximum_fusion.refs_0_), channel_id=1, source_target_pairs={{0,8},{1,9},{2,10},{3,11},{4,12},{5,13},{6,14},{7,15},{8,16},{9,17... | collective-permute-start | bytes 6152 | tf_op jit(solution)/shard_map/ppermute | solution.py:340
  14.3 4.0 %collective-permute-start.15 = (bf16[8,128]{1,0:T(8,128)(2,1)S(1)}, bf16[8,128]{1,0:T(8,128)(2,1)S(1)}, u32[]{:S(2)}, u32[]{:S(2)}) collective-permute-start(bf16[8,128]{1,0:T(8,128)(2,1)S(1)} %pad_maximum_fusion.refs_0_), channel_id=1, source_target_pairs={{0,12},{1,13},{2,14},{3,15},{4,16},{5,17},{6,18},{7,19},{8,20},{9,... | collective-permute-start | bytes 6152 | tf_op jit(solution)/shard_map/ppermute | solution.py:340
  18.3 0.5 collective-permute-start.16
  18.9 4.9 %collective-permute-start.17 = (bf16[8,128]{1,0:T(8,128)(2,1)S(1)}, bf16[8,128]{1,0:T(8,128)(2,1)S(1)}, u32[]{:S(2)}, u32[]{:S(2)}) collective-permute-start(bf16[8,128]{1,0:T(8,128)(2,1)S(1)} %pad_maximum_fusion.refs_0_), channel_id=1, source_target_pairs={{0,20},{1,21},{2,22},{3,23},{4,24},{5,25},{6,26},{7,27},{8,28},{9,... | collective-permute-start | bytes 6152 | tf_op jit(solution)/shard_map/ppermute | solution.py:340
  23.8 0.0 collective-permute-done.13.refs_1_
  23.8 2.7 %collective-permute-start.18 = (bf16[8,128]{1,0:T(8,128)(2,1)S(1)}, bf16[8,128]{1,0:T(8,128)(2,1)S(1)}, u32[]{:S(2)}, u32[]{:S(2)}) collective-permute-start(bf16[8,128]{1,0:T(8,128)(2,1)S(1)} %pad_maximum_fusion.refs_0_), channel_id=1, source_target_pairs={{0,24},{1,25},{2,26},{3,27},{4,28},{5,29},{6,30},{7,31},{8,0},{9,1... | collective-permute-start | bytes 6152 | tf_op jit(solution)/shard_map/ppermute | solution.py:340
  26.5 0.0 collective-permute-done.14.refs_2_
  26.5 1.0 collective-permute-start.19
  27.5 0.0 collective-permute-done.15.refs_3_
  27.5 0.0 collective-permute-done.16.refs_4_
  27.5 0.0 collective-permute-done.17.refs_5_
  27.5 0.8 collective-permute-done.18.refs_6_
  28.3 1.8 %collective-permute-done.19.refs_7_ = bf16[8,128]{1,0:T(8,128)(2,1)S(1)} collective-permute-done((bf16[8,128]{1,0:T(8,128)(2,1)S(1)}, bf16[8,128]{1,0:T(8,128)(2,1)S(1)}, u32[]{:S(2)}, u32[]{:S(2)}) %collective-permute-start.19) | collective-permute-done | bytes 2080 | tf_op jit(solution)/shard_map/ppermute | solution.py:340
  30.1 0.8 router.1
  30.8 4.5 %all-to-all-start.1 = ((bf16[8,2,4096]{2,1,0:T(2,128)(2,1)}), bf16[8,2,4096]{2,1,0:T(2,128)(2,1)S(1)}, u32[]{:S(2)}, u32[]{:S(2)}) async-start(bf16[8,2,4096]{2,1,0:T(2,128)(2,1)} %router.1), calls=%async_computation.1 | async-start | bytes 262144 | tf_op jit(solution)/shard_map/all_to_all | solution.py:370
  35.3 3.6 %packed.1 = bf16[32,2,128,128]{3,2,1,0:T(8,128)(2,1)} custom-call(f32[2,32,200,128]{3,2,1,0:T(8,128)} %bitcast.5, bf16[2,32,200,128]{3,2,1,0:T(8,128)(2,1)} %bitcast.7), custom_call_target="tpu_custom_call" | custom-call | tf_op jit(solution)/shard_map/packed/pallas_call | solution.py:56
  38.9 2.5 %all-to-all-done.1 = bf16[8,2,4096]{2,1,0:T(2,128)(2,1)S(1)} async-done(((bf16[8,2,4096]{2,1,0:T(2,128)(2,1)}), bf16[8,2,4096]{2,1,0:T(2,128)(2,1)S(1)}, u32[]{:S(2)}, u32[]{:S(2)}) %all-to-all-start.1) | async-done | bytes 131104 | tf_op jit(solution)/shard_map/all_to_all | solution.py:370
  41.4 6.3 %all-to-all-start = ((bf16[32,2,128,128]{3,2,1,0:T(8,128)(2,1)}), bf16[32,2,128,128]{3,2,1,0:T(8,128)(2,1)S(1)}, u32[]{:S(2)}, u32[]{:S(2)}) async-start(bf16[32,2,128,128]{3,2,1,0:T(8,128)(2,1)} %packed.1), calls=%async_computation | async-start | bytes 4194304 | tf_op jit(solution)/shard_map/all_to_all | solution.py:355
  47.8 4.0 %sorted.1 = (bf16[8,144,128]{2,1,0:T(8,128)(2,1)}, bf16[8,144,128]{2,1,0:T(8,128)(2,1)}, bf16[8,144,128]{2,1,0:T(8,128)(2,1)}, bf16[8,144,128]{2,1,0:T(8,128)(2,1)}) custom-call(s32[32]{0:T(128)S(1)} %and_or_fusion.targets, f32[2,32,200,128]{3,2,1,0:T(8,128)} %bitcast.6, bf16[2,32,200,128]{3,2,1,0:T(8,128)(2,1)} %bitcast.8), custom_call_target="tpu_custom_call" | custom-call | tf_op jit(solution)/shard_map/sorted/pallas_call | solution.py:109
  51.7 0.3 collective-permute-start
  52.0 2.7 %collective-permute-start.1 = (bf16[8,144,128]{2,1,0:T(8,128)(2,1)}, bf16[8,144,128]{2,1,0:T(8,128)(2,1)S(1)}, u32[]{:S(2)}, u32[]{:S(2)}) collective-permute-start(bf16[8,144,128]{2,1,0:T(8,128)(2,1)} %get-tuple-element.22), channel_id=1, source_target_pairs={{0,2},{1,3},{2,0},{3,1},{4,6},{5,7},{6,4},{7,5},{8,10},{9,11},{10,... | collective-permute-start | bytes 884744 | tf_op jit(solution)/shard_map/ppermute | solution.py:340
  54.7 0.0 collective-permute-start.2
  54.7 19.5 %collective-permute-done.refs_1_ = bf16[8,144,128]{2,1,0:T(8,128)(2,1)S(1)} collective-permute-done((bf16[8,144,128]{2,1,0:T(8,128)(2,1)}, bf16[8,144,128]{2,1,0:T(8,128)(2,1)S(1)}, u32[]{:S(2)}, u32[]{:S(2)}) %collective-permute-start) | collective-permute-done | bytes 294944 | tf_op jit(solution)/shard_map/ppermute | solution.py:340
  74.3 0.0 collective-permute-done.1.refs_2_
  74.3 8.4 %collective-permute-done.2.refs_3_ = bf16[8,144,128]{2,1,0:T(8,128)(2,1)S(1)} collective-permute-done((bf16[8,144,128]{2,1,0:T(8,128)(2,1)}, bf16[8,144,128]{2,1,0:T(8,128)(2,1)S(1)}, u32[]{:S(2)}, u32[]{:S(2)}) %collective-permute-start.2) | collective-permute-done | bytes 294944 | tf_op jit(solution)/shard_map/ppermute | solution.py:340
  82.7 0.0 copy-start
  82.7 1.0 copy-done
  83.6 1.3 %turned.1 = (bf16[4,144,128]{2,1,0:T(8,128)(2,1)S(1)}, bf16[4,144,128]{2,1,0:T(8,128)(2,1)}, bf16[4,144,128]{2,1,0:T(8,128)(2,1)}, bf16[4,144,128]{2,1,0:T(8,128...) custom-call(bf16[8,144,128]{2,1,0:T(8,128)(2,1)S(1)} %copy-done, ...), custom_call_target="tpu_custom_call" | custom-call | tf_op jit(solution)/shard_map/turned/pallas_call | solution.py:145
  84.9 0.3 collective-permute-start.3
  85.2 4.7 %collective-permute-start.4 = (bf16[4,144,128]{2,1,0:T(8,128)(2,1)}, bf16[4,144,128]{2,1,0:T(8,128)(2,1)S(1)}, u32[]{:S(2)}, u32[]{:S(2)}) collective-permute-start(bf16[4,144,128]{2,1,0:T(8,128)(2,1)} %get-tuple-element.26), channel_id=1, source_target_pairs={{0,12},{1,13},{2,14},{3,15},{4,16},{5,17},{6,18},{7,19},{8,20},{9,... | collective-permute-start | bytes 442376 | tf_op jit(solution)/shard_map/ppermute | solution.py:340
  90.0 0.4 collective-permute-start.5
  90.4 4.3 %collective-permute-start.6 = (bf16[4,144,128]{2,1,0:T(8,128)(2,1)}, bf16[4,144,128]{2,1,0:T(8,128)(2,1)S(1)}, u32[]{:S(2)}, u32[]{:S(2)}) collective-permute-start(bf16[4,144,128]{2,1,0:T(8,128)(2,1)} %get-tuple-element.28), channel_id=1, source_target_pairs={{0,20},{1,21},{2,22},{3,23},{4,24},{5,25},{6,26},{7,27},{8,28},{9,... | collective-permute-start | bytes 442376 | tf_op jit(solution)/shard_map/ppermute | solution.py:340
  94.7 3.9 %collective-permute-start.7 = (bf16[4,144,128]{2,1,0:T(8,128)(2,1)}, bf16[4,144,128]{2,1,0:T(8,128)(2,1)S(1)}, u32[]{:S(2)}, u32[]{:S(2)}) collective-permute-start(bf16[4,144,128]{2,1,0:T(8,128)(2,1)} %get-tuple-element.29), channel_id=1, source_target_pairs={{0,24},{1,25},{2,26},{3,27},{4,28},{5,29},{6,30},{7,31},{8,0},{9,1... | collective-permute-start | bytes 442376 | tf_op jit(solution)/shard_map/ppermute | solution.py:340
  98.5 6.3 %collective-permute-done.3.refs_1_.refs_2_ = bf16[4,144,128]{2,1,0:T(8,128)(2,1)S(1)} collective-permute-done((bf16[4,144,128]{2,1,0:T(8,128)(2,1)}, bf16[4,144,128]{2,1,0:T(8,128)(2,1)S(1)}, u32[]{:S(2)}, u32[]{:S(2)}) %collective-permute-start.3) | collective-permute-done | bytes 147488 | tf_op jit(solution)/shard_map/ppermute | solution.py:340
  104.8 2.8 %collective-permute-start.8 = (bf16[4,144,128]{2,1,0:T(8,128)(2,1)}, bf16[4,144,128]{2,1,0:T(8,128)(2,1)S(1)}, u32[]{:S(2)}, u32[]{:S(2)}) collective-permute-start(bf16[4,144,128]{2,1,0:T(8,128)(2,1)} %get-tuple-element.30), channel_id=1, source_target_pairs={{0,4},{1,5},{2,6},{3,7},{4,8},{5,9},{6,10},{7,11},{8,12},{9,13},{1... | collective-permute-start | bytes 442376 | tf_op jit(solution)/shard_map/ppermute | solution.py:340
  107.6 11.6 %collective-permute-done.4.refs_2_.refs_3_ = bf16[4,144,128]{2,1,0:T(8,128)(2,1)S(1)} collective-permute-done((bf16[4,144,128]{2,1,0:T(8,128)(2,1)}, bf16[4,144,128]{2,1,0:T(8,128)(2,1)S(1)}, u32[]{:S(2)}, u32[]{:S(2)}) %collective-permute-start.4) | collective-permute-done | bytes 147488 | tf_op jit(solution)/shard_map/ppermute | solution.py:340
  119.1 0.0 collective-permute-start.9
  119.2 0.7 reshape.18
  119.9 0.0 collective-permute-done.5.refs_3_.refs_4_
  119.9 0.0 collective-permute-done.6.refs_4_.refs_5_
  119.9 0.0 collective-permute-done.7.refs_5_.refs_6_
  119.9 0.1 middle.1.middle_ref
  120.0 0.0 all-to-all-done.parts_ref
  120.0 1.6 %first.1 = (bf16[2,200,4096]{2,1,0:T(8,128)(2,1)}, f32[2,128,128]{2,1,0:T(8,128)S(1)}) custom-call(bf16[32,2,128,128]{3,2,1,0:T(8,128)(2,1)S(1)} %all-to-all-done.parts_ref), custom_call_target="tpu_custom_call" | custom-call | tf_op jit(solution)/shard_map/first/pallas_call | solution.py:194
  121.5 0.0 collective-permute-done.8.refs_1_
  121.5 3.0 %collective-permute-done.9.refs_7_ = bf16[4,144,128]{2,1,0:T(8,128)(2,1)S(1)} collective-permute-done((bf16[4,144,128]{2,1,0:T(8,128)(2,1)}, bf16[4,144,128]{2,1,0:T(8,128)(2,1)S(1)}, u32[]{:S(2)}, u32[]{:S(2)}) %collective-permute-start.9) | collective-permute-done | bytes 147488 | tf_op jit(solution)/shard_map/ppermute | solution.py:340
  124.5 1.2 last.1
  (2 shorter events, 0.0 us)
Async XLA Ops:
  1.3 3.6 %collective-permute-start.10 = (bf16[2,128]{1,0:T(2,128)(2,1)S(1)}, bf16[2,128]{1,0:T(2,128)(2,1)S(1)}, u32[]{:S(2)}, u32[]{:S(2)}) collective-permute-start(bf16[2,128]{1,0:T(2,128)(2,1)S(1)} %fusion), channel_id=1, source_target_pairs={{0,1},{1,2},{2,3},{3,0},{4,5},{5,6},{6,7},{7,4},{8,9},{9,10},{10,1... | collective-permute-start | bytes 1544 | tf_op jit(solution)/shard_map/ppermute | solution.py:340
  3.5 5.1 %collective-permute-start.11 = (bf16[2,128]{1,0:T(2,128)(2,1)S(1)}, bf16[2,128]{1,0:T(2,128)(2,1)S(1)}, u32[]{:S(2)}, u32[]{:S(2)}) collective-permute-start(bf16[2,128]{1,0:T(2,128)(2,1)S(1)} %fusion), channel_id=1, source_target_pairs={{0,2},{1,3},{2,0},{3,1},{4,6},{5,7},{6,4},{7,5},{8,10},{9,11},{10,... | collective-permute-start | bytes 1544 | tf_op jit(solution)/shard_map/ppermute | solution.py:340
  4.2 4.8 %collective-permute-start.12 = (bf16[2,128]{1,0:T(2,128)(2,1)S(1)}, bf16[2,128]{1,0:T(2,128)(2,1)S(1)}, u32[]{:S(2)}, u32[]{:S(2)}) collective-permute-start(bf16[2,128]{1,0:T(2,128)(2,1)S(1)} %fusion), channel_id=1, source_target_pairs={{0,3},{1,0},{2,1},{3,2},{4,7},{5,4},{6,5},{7,6},{8,11},{9,8},{10,9... | collective-permute-start | bytes 1544 | tf_op jit(solution)/shard_map/ppermute | solution.py:340
  9.0 14.8 %collective-permute-start.13 = (bf16[8,128]{1,0:T(8,128)(2,1)S(1)}, bf16[8,128]{1,0:T(8,128)(2,1)S(1)}, u32[]{:S(2)}, u32[]{:S(2)}) collective-permute-start(bf16[8,128]{1,0:T(8,128)(2,1)S(1)} %pad_maximum_fusion.refs_0_), channel_id=1, source_target_pairs={{0,4},{1,5},{2,6},{3,7},{4,8},{5,9},{6,10},{7,11},{8,12},{9,13},{1... | collective-permute-start | bytes 6152 | tf_op jit(solution)/shard_map/ppermute | solution.py:340
  11.0 15.5 %collective-permute-start.14 = (bf16[8,128]{1,0:T(8,128)(2,1)S(1)}, bf16[8,128]{1,0:T(8,128)(2,1)S(1)}, u32[]{:S(2)}, u32[]{:S(2)}) collective-permute-start(bf16[8,128]{1,0:T(8,128)(2,1)S(1)} %pad_maximum_fusion.refs_0_), channel_id=1, source_target_pairs={{0,8},{1,9},{2,10},{3,11},{4,12},{5,13},{6,14},{7,15},{8,16},{9,17... | collective-permute-start | bytes 6152 | tf_op jit(solution)/shard_map/ppermute | solution.py:340
  14.3 13.2 %collective-permute-start.15 = (bf16[8,128]{1,0:T(8,128)(2,1)S(1)}, bf16[8,128]{1,0:T(8,128)(2,1)S(1)}, u32[]{:S(2)}, u32[]{:S(2)}) collective-permute-start(bf16[8,128]{1,0:T(8,128)(2,1)S(1)} %pad_maximum_fusion.refs_0_), channel_id=1, source_target_pairs={{0,12},{1,13},{2,14},{3,15},{4,16},{5,17},{6,18},{7,19},{8,20},{9,... | collective-permute-start | bytes 6152 | tf_op jit(solution)/shard_map/ppermute | solution.py:340
  18.3 9.2 %collective-permute-start.16 = (bf16[8,128]{1,0:T(8,128)(2,1)S(1)}, bf16[8,128]{1,0:T(8,128)(2,1)S(1)}, u32[]{:S(2)}, u32[]{:S(2)}) collective-permute-start(bf16[8,128]{1,0:T(8,128)(2,1)S(1)} %pad_maximum_fusion.refs_0_), channel_id=1, source_target_pairs={{0,16},{1,17},{2,18},{3,19},{4,20},{5,21},{6,22},{7,23},{8,24},{9,... | collective-permute-start | bytes 6152 | tf_op jit(solution)/shard_map/ppermute | solution.py:340
  18.9 8.6 %collective-permute-start.17 = (bf16[8,128]{1,0:T(8,128)(2,1)S(1)}, bf16[8,128]{1,0:T(8,128)(2,1)S(1)}, u32[]{:S(2)}, u32[]{:S(2)}) collective-permute-start(bf16[8,128]{1,0:T(8,128)(2,1)S(1)} %pad_maximum_fusion.refs_0_), channel_id=1, source_target_pairs={{0,20},{1,21},{2,22},{3,23},{4,24},{5,25},{6,26},{7,27},{8,28},{9,... | collective-permute-start | bytes 6152 | tf_op jit(solution)/shard_map/ppermute | solution.py:340
  23.8 4.5 %collective-permute-start.18 = (bf16[8,128]{1,0:T(8,128)(2,1)S(1)}, bf16[8,128]{1,0:T(8,128)(2,1)S(1)}, u32[]{:S(2)}, u32[]{:S(2)}) collective-permute-start(bf16[8,128]{1,0:T(8,128)(2,1)S(1)} %pad_maximum_fusion.refs_0_), channel_id=1, source_target_pairs={{0,24},{1,25},{2,26},{3,27},{4,28},{5,29},{6,30},{7,31},{8,0},{9,1... | collective-permute-start | bytes 6152 | tf_op jit(solution)/shard_map/ppermute | solution.py:340
  26.5 3.6 %collective-permute-start.19 = (bf16[8,128]{1,0:T(8,128)(2,1)S(1)}, bf16[8,128]{1,0:T(8,128)(2,1)S(1)}, u32[]{:S(2)}, u32[]{:S(2)}) collective-permute-start(bf16[8,128]{1,0:T(8,128)(2,1)S(1)} %pad_maximum_fusion.refs_0_), channel_id=1, source_target_pairs={{0,28},{1,29},{2,30},{3,31},{4,0},{5,1},{6,2},{7,3},{8,4},{9,5},{1... | collective-permute-start | bytes 6152 | tf_op jit(solution)/shard_map/ppermute | solution.py:340
  30.8 10.6 %all-to-all-start.1 = ((bf16[8,2,4096]{2,1,0:T(2,128)(2,1)}), bf16[8,2,4096]{2,1,0:T(2,128)(2,1)S(1)}, u32[]{:S(2)}, u32[]{:S(2)}) async-start(bf16[8,2,4096]{2,1,0:T(2,128)(2,1)} %router.1), calls=%async_computation.1 | async-start | bytes 262144 | tf_op jit(solution)/shard_map/all_to_all | solution.py:370
  41.4 78.5 %all-to-all-start = ((bf16[32,2,128,128]{3,2,1,0:T(8,128)(2,1)}), bf16[32,2,128,128]{3,2,1,0:T(8,128)(2,1)S(1)}, u32[]{:S(2)}, u32[]{:S(2)}) async-start(bf16[32,2,128,128]{3,2,1,0:T(8,128)(2,1)} %packed.1), calls=%async_computation | async-start | bytes 4194304 | tf_op jit(solution)/shard_map/all_to_all | solution.py:355
  51.7 22.5 %collective-permute-start = (bf16[8,144,128]{2,1,0:T(8,128)(2,1)}, bf16[8,144,128]{2,1,0:T(8,128)(2,1)S(1)}, u32[]{:S(2)}, u32[]{:S(2)}) collective-permute-start(bf16[8,144,128]{2,1,0:T(8,128)(2,1)} %get-tuple-element.21), channel_id=1, source_target_pairs={{0,1},{1,2},{2,3},{3,0},{4,5},{5,6},{6,7},{7,4},{8,9},{9,10},{10,1... | collective-permute-start | bytes 884744 | tf_op jit(solution)/shard_map/ppermute | solution.py:340
  52.0 22.2 %collective-permute-start.1 = (bf16[8,144,128]{2,1,0:T(8,128)(2,1)}, bf16[8,144,128]{2,1,0:T(8,128)(2,1)S(1)}, u32[]{:S(2)}, u32[]{:S(2)}) collective-permute-start(bf16[8,144,128]{2,1,0:T(8,128)(2,1)} %get-tuple-element.22), channel_id=1, source_target_pairs={{0,2},{1,3},{2,0},{3,1},{4,6},{5,7},{6,4},{7,5},{8,10},{9,11},{10,... | collective-permute-start | bytes 884744 | tf_op jit(solution)/shard_map/ppermute | solution.py:340
  54.7 27.9 %collective-permute-start.2 = (bf16[8,144,128]{2,1,0:T(8,128)(2,1)}, bf16[8,144,128]{2,1,0:T(8,128)(2,1)S(1)}, u32[]{:S(2)}, u32[]{:S(2)}) collective-permute-start(bf16[8,144,128]{2,1,0:T(8,128)(2,1)} %get-tuple-element.23), channel_id=1, source_target_pairs={{0,3},{1,0},{2,1},{3,2},{4,7},{5,4},{6,5},{7,6},{8,11},{9,8},{10,9... | collective-permute-start | bytes 884744 | tf_op jit(solution)/shard_map/ppermute | solution.py:340
  82.7 1.0 copy-start
  84.9 19.9 %collective-permute-start.3 = (bf16[4,144,128]{2,1,0:T(8,128)(2,1)}, bf16[4,144,128]{2,1,0:T(8,128)(2,1)S(1)}, u32[]{:S(2)}, u32[]{:S(2)}) collective-permute-start(bf16[4,144,128]{2,1,0:T(8,128)(2,1)} %get-tuple-element.25), channel_id=1, source_target_pairs={{0,8},{1,9},{2,10},{3,11},{4,12},{5,13},{6,14},{7,15},{8,16},{9,17... | collective-permute-start | bytes 442376 | tf_op jit(solution)/shard_map/ppermute | solution.py:340
  85.2 33.9 %collective-permute-start.4 = (bf16[4,144,128]{2,1,0:T(8,128)(2,1)}, bf16[4,144,128]{2,1,0:T(8,128)(2,1)S(1)}, u32[]{:S(2)}, u32[]{:S(2)}) collective-permute-start(bf16[4,144,128]{2,1,0:T(8,128)(2,1)} %get-tuple-element.26), channel_id=1, source_target_pairs={{0,12},{1,13},{2,14},{3,15},{4,16},{5,17},{6,18},{7,19},{8,20},{9,... | collective-permute-start | bytes 442376 | tf_op jit(solution)/shard_map/ppermute | solution.py:340
  90.0 29.9 %collective-permute-start.5 = (bf16[4,144,128]{2,1,0:T(8,128)(2,1)}, bf16[4,144,128]{2,1,0:T(8,128)(2,1)S(1)}, u32[]{:S(2)}, u32[]{:S(2)}) collective-permute-start(bf16[4,144,128]{2,1,0:T(8,128)(2,1)} %get-tuple-element.27), channel_id=1, source_target_pairs={{0,16},{1,17},{2,18},{3,19},{4,20},{5,21},{6,22},{7,23},{8,24},{9,... | collective-permute-start | bytes 442376 | tf_op jit(solution)/shard_map/ppermute | solution.py:340
  90.4 29.5 %collective-permute-start.6 = (bf16[4,144,128]{2,1,0:T(8,128)(2,1)}, bf16[4,144,128]{2,1,0:T(8,128)(2,1)S(1)}, u32[]{:S(2)}, u32[]{:S(2)}) collective-permute-start(bf16[4,144,128]{2,1,0:T(8,128)(2,1)} %get-tuple-element.28), channel_id=1, source_target_pairs={{0,20},{1,21},{2,22},{3,23},{4,24},{5,25},{6,26},{7,27},{8,28},{9,... | collective-permute-start | bytes 442376 | tf_op jit(solution)/shard_map/ppermute | solution.py:340
  94.7 25.2 %collective-permute-start.7 = (bf16[4,144,128]{2,1,0:T(8,128)(2,1)}, bf16[4,144,128]{2,1,0:T(8,128)(2,1)S(1)}, u32[]{:S(2)}, u32[]{:S(2)}) collective-permute-start(bf16[4,144,128]{2,1,0:T(8,128)(2,1)} %get-tuple-element.29), channel_id=1, source_target_pairs={{0,24},{1,25},{2,26},{3,27},{4,28},{5,29},{6,30},{7,31},{8,0},{9,1... | collective-permute-start | bytes 442376 | tf_op jit(solution)/shard_map/ppermute | solution.py:340
  104.8 16.7 %collective-permute-start.8 = (bf16[4,144,128]{2,1,0:T(8,128)(2,1)}, bf16[4,144,128]{2,1,0:T(8,128)(2,1)S(1)}, u32[]{:S(2)}, u32[]{:S(2)}) collective-permute-start(bf16[4,144,128]{2,1,0:T(8,128)(2,1)} %get-tuple-element.30), channel_id=1, source_target_pairs={{0,4},{1,5},{2,6},{3,7},{4,8},{5,9},{6,10},{7,11},{8,12},{9,13},{1... | collective-permute-start | bytes 442376 | tf_op jit(solution)/shard_map/ppermute | solution.py:340
  119.1 5.4 %collective-permute-start.9 = (bf16[4,144,128]{2,1,0:T(8,128)(2,1)}, bf16[4,144,128]{2,1,0:T(8,128)(2,1)S(1)}, u32[]{:S(2)}, u32[]{:S(2)}) collective-permute-start(bf16[4,144,128]{2,1,0:T(8,128)(2,1)} %get-tuple-element.31), channel_id=1, source_target_pairs={{0,28},{1,29},{2,30},{3,31},{4,0},{5,1},{6,2},{7,3},{8,4},{9,5},{1... | collective-permute-start | bytes 442376 | tf_op jit(solution)/shard_map/ppermute | solution.py:340

commit v4 on v3

--- a/solution.py
+++ b/solution.py
@@ -85,7 +85,7 @@
         )
 
     def copy_out(i):
-        return pltpu.make_async_copy(out_vmem.at[i], outs[i], out_sem.at[i])
+        return pltpu.make_async_copy(out_vmem.at[i - 1], outs[i], out_sem.at[i - 1])
 
     for s in range(shards):
         for copy in copies(s):
@@ -95,11 +95,13 @@
             for copy in copies(i * RING + j):
                 copy.wait()
             for expert in range(experts):
-                out_vmem[i, j, pl.ds(expert * rows, rows)] = merged(
+                kept = outs[0] if i == 0 else out_vmem.at[i - 1]
+                kept[j, pl.ds(expert * rows, rows)] = merged(
                     master_vmem[expert, i * RING + j], second_vmem[expert, i * RING + j]
                 )
-        copy_out(i).start()
-    for i in range(CROSS):
+        if i:
+            copy_out(i).start()
+    for i in range(1, CROSS):
         copy_out(i).wait()
 
 
@@ -109,15 +111,15 @@
     return pl.pallas_call(
         sorted_kernel,
         in_specs=[pl.BlockSpec(memory_space=pltpu.SMEM)] + [pl.BlockSpec(memory_space=pltpu.HBM)] * 2,
-        out_specs=[pl.BlockSpec(memory_space=pltpu.HBM)] * CROSS,
-        out_shape=[pltpu.HBM(block, jnp.bfloat16)] * CROSS,
+        out_specs=[pl.BlockSpec(memory_space=pltpu.VMEM)] + [pl.BlockSpec(memory_space=pltpu.HBM)] * (CROSS - 1),
+        out_shape=[pltpu.VMEM(block, jnp.bfloat16)] + [pltpu.HBM(block, jnp.bfloat16)] * (CROSS - 1),
         scratch_shapes=[
             pltpu.VMEM((experts, shards, rows, lanes), jnp.float32),
             pltpu.VMEM((experts, shards, rows, lanes), jnp.bfloat16),
-            pltpu.VMEM((CROSS, *block), jnp.bfloat16),
+            pltpu.VMEM((CROSS - 1, *block), jnp.bfloat16),
             pltpu.SemaphoreType.DMA((shards,)),
             pltpu.SemaphoreType.DMA((shards,)),
-            pltpu.SemaphoreType.DMA((CROSS,)),
+            pltpu.SemaphoreType.DMA((CROSS - 1,)),
         ],
         compiler_params=pltpu.CompilerParams(vmem_limit_bytes=VMEM_LIMIT),
         name="sorted",

time: 126 us -> 126 us (level)
  no operation moved by 1% of the time
where the time goes in v4:
time: 126 us
  waiting for transfers between devices  59.4 us (47%)
  starting transfers between devices  51.7 us (41%)
  Pallas kernels  12.5 us (10%)
    ppermute x20, waiting for transfers between devices, moved(): return lax.ppermute(x, 'shard', pairs)  56.9 us
    ppermute x20, starting transfers between devices, moved(): return lax.ppermute(x, 'shard', pairs)  40.9 us
    all_to_all x1, starting transfers between devices, body(): received = lax.all_to_all(sent, 'shard', 0, 0, tiled=True)  6.32 us
    all_to_all x1, starting transfers between devices, body(): gathered = lax.all_to_all(copies, 'expert', 0, 0, tiled=True)  4.48 us
    pallas_call x1, Pallas kernels, sorted_by_cross(): pl.pallas_call(sorted_kernel, in_specs=[pl.BlockSpec(memory_space=pltpu.S...  3.96 us
    pallas_call x1, Pallas kernels, packed(): pl.pallas_call(packed_kernel, in_specs=[pl.BlockSpec(memory_space=pltpu.H...  3.61 us
  transfers between devices with their start and end apart: 22, of which 11 were waited for; matrix products, arithmetic and copies ran while one was open for 1% of the time, Pallas kernels for 8%

profile of v4, /device:TPU:6, one launch (start us, length us, event | category | flops | bytes accessed | tf_op | source)
XLA Modules:
  0.0 125.9 jit_solution(4570627478005385202)
XLA Ops:
  0.6 0.7 fusion
  1.3 2.2 %collective-permute-start.10 = (bf16[2,128]{1,0:T(2,128)(2,1)S(1)}, bf16[2,128]{1,0:T(2,128)(2,1)S(1)}, u32[]{:S(2)}, u32[]{:S(2)}) collective-permute-start(bf16[2,128]{1,0:T(2,128)(2,1)S(1)} %fusion), channel_id=1, source_target_pairs={{0,1},{1,2},{2,3},{3,0},{4,5},{5,6},{6,7},{7,4},{8,9},{9,10},{10,1... | collective-permute-start | bytes 1544 | tf_op jit(solution)/shard_map/ppermute | solution.py:342
  3.5 0.7 collective-permute-start.11
  4.2 0.1 collective-permute-start.12
  4.4 0.5 collective-permute-done.10
  4.9 3.7 %collective-permute-done.11 = bf16[2,128]{1,0:T(2,128)(2,1)S(1)} collective-permute-done((bf16[2,128]{1,0:T(2,128)(2,1)S(1)}, bf16[2,128]{1,0:T(2,128)(2,1)S(1)}, u32[]{:S(2)}, u32[]{:S(2)}) %collective-permute-start.11) | collective-permute-done | bytes 544 | tf_op jit(solution)/shard_map/ppermute | solution.py:342
  8.6 0.4 collective-permute-done.12
  9.0 2.0 %collective-permute-start.13 = (bf16[8,128]{1,0:T(8,128)(2,1)S(1)}, bf16[8,128]{1,0:T(8,128)(2,1)S(1)}, u32[]{:S(2)}, u32[]{:S(2)}) collective-permute-start(bf16[8,128]{1,0:T(8,128)(2,1)S(1)} %pad_maximum_fusion.refs_0_), channel_id=1, source_target_pairs={{0,4},{1,5},{2,6},{3,7},{4,8},{5,9},{6,10},{7,11},{8,12},{9,13},{1... | collective-permute-start | bytes 6152 | tf_op jit(solution)/shard_map/ppermute | solution.py:342
  11.0 3.3 %collective-permute-start.14 = (bf16[8,128]{1,0:T(8,128)(2,1)S(1)}, bf16[8,128]{1,0:T(8,128)(2,1)S(1)}, u32[]{:S(2)}, u32[]{:S(2)}) collective-permute-start(bf16[8,128]{1,0:T(8,128)(2,1)S(1)} %pad_maximum_fusion.refs_0_), channel_id=1, source_target_pairs={{0,8},{1,9},{2,10},{3,11},{4,12},{5,13},{6,14},{7,15},{8,16},{9,17... | collective-permute-start | bytes 6152 | tf_op jit(solution)/shard_map/ppermute | solution.py:342
  14.3 4.0 %collective-permute-start.15 = (bf16[8,128]{1,0:T(8,128)(2,1)S(1)}, bf16[8,128]{1,0:T(8,128)(2,1)S(1)}, u32[]{:S(2)}, u32[]{:S(2)}) collective-permute-start(bf16[8,128]{1,0:T(8,128)(2,1)S(1)} %pad_maximum_fusion.refs_0_), channel_id=1, source_target_pairs={{0,12},{1,13},{2,14},{3,15},{4,16},{5,17},{6,18},{7,19},{8,20},{9,... | collective-permute-start | bytes 6152 | tf_op jit(solution)/shard_map/ppermute | solution.py:342
  18.3 0.5 collective-permute-start.16
  18.9 4.9 %collective-permute-start.17 = (bf16[8,128]{1,0:T(8,128)(2,1)S(1)}, bf16[8,128]{1,0:T(8,128)(2,1)S(1)}, u32[]{:S(2)}, u32[]{:S(2)}) collective-permute-start(bf16[8,128]{1,0:T(8,128)(2,1)S(1)} %pad_maximum_fusion.refs_0_), channel_id=1, source_target_pairs={{0,20},{1,21},{2,22},{3,23},{4,24},{5,25},{6,26},{7,27},{8,28},{9,... | collective-permute-start | bytes 6152 | tf_op jit(solution)/shard_map/ppermute | solution.py:342
  23.8 0.0 collective-permute-done.13.refs_1_
  23.8 2.7 %collective-permute-start.18 = (bf16[8,128]{1,0:T(8,128)(2,1)S(1)}, bf16[8,128]{1,0:T(8,128)(2,1)S(1)}, u32[]{:S(2)}, u32[]{:S(2)}) collective-permute-start(bf16[8,128]{1,0:T(8,128)(2,1)S(1)} %pad_maximum_fusion.refs_0_), channel_id=1, source_target_pairs={{0,24},{1,25},{2,26},{3,27},{4,28},{5,29},{6,30},{7,31},{8,0},{9,1... | collective-permute-start | bytes 6152 | tf_op jit(solution)/shard_map/ppermute | solution.py:342
  26.5 0.0 collective-permute-done.14.refs_2_
  26.5 1.0 collective-permute-start.19
  27.5 0.0 collective-permute-done.15.refs_3_
  27.5 0.0 collective-permute-done.16.refs_4_
  27.5 0.0 collective-permute-done.17.refs_5_
  27.5 0.8 collective-permute-done.18.refs_6_
  28.3 1.8 %collective-permute-done.19.refs_7_ = bf16[8,128]{1,0:T(8,128)(2,1)S(1)} collective-permute-done((bf16[8,128]{1,0:T(8,128)(2,1)S(1)}, bf16[8,128]{1,0:T(8,128)(2,1)S(1)}, u32[]{:S(2)}, u32[]{:S(2)}) %collective-permute-start.19) | collective-permute-done | bytes 2080 | tf_op jit(solution)/shard_map/ppermute | solution.py:342
  30.1 0.8 router.1
  30.8 4.5 %all-to-all-start.1 = ((bf16[8,2,4096]{2,1,0:T(2,128)(2,1)}), bf16[8,2,4096]{2,1,0:T(2,128)(2,1)S(1)}, u32[]{:S(2)}, u32[]{:S(2)}) async-start(bf16[8,2,4096]{2,1,0:T(2,128)(2,1)} %router.1), calls=%async_computation.1 | async-start | bytes 262144 | tf_op jit(solution)/shard_map/all_to_all | solution.py:372
  35.3 3.6 %packed.1 = bf16[32,2,128,128]{3,2,1,0:T(8,128)(2,1)} custom-call(f32[2,32,200,128]{3,2,1,0:T(8,128)} %bitcast.5, bf16[2,32,200,128]{3,2,1,0:T(8,128)(2,1)} %bitcast.7), custom_call_target="tpu_custom_call" | custom-call | tf_op jit(solution)/shard_map/packed/pallas_call | solution.py:56
  38.9 2.5 %all-to-all-done.1 = bf16[8,2,4096]{2,1,0:T(2,128)(2,1)S(1)} async-done(((bf16[8,2,4096]{2,1,0:T(2,128)(2,1)}), bf16[8,2,4096]{2,1,0:T(2,128)(2,1)S(1)}, u32[]{:S(2)}, u32[]{:S(2)}) %all-to-all-start.1) | async-done | bytes 131104 | tf_op jit(solution)/shard_map/all_to_all | solution.py:372
  41.4 6.3 %all-to-all-start = ((bf16[32,2,128,128]{3,2,1,0:T(8,128)(2,1)}), bf16[32,2,128,128]{3,2,1,0:T(8,128)(2,1)S(1)}, u32[]{:S(2)}, u32[]{:S(2)}) async-start(bf16[32,2,128,128]{3,2,1,0:T(8,128)(2,1)} %packed.1), calls=%async_computation | async-start | bytes 4194304 | tf_op jit(solution)/shard_map/all_to_all | solution.py:357
  47.8 4.0 %sorted.1 = (bf16[8,144,128]{2,1,0:T(8,128)(2,1)S(1)}, bf16[8,144,128]{2,1,0:T(8,128)(2,1)}, bf16[8,144,128]{2,1,0:T(8,128)(2,1)}, bf16[8,144,128]{2,1,0:T(8,128)(2,1)}) custom-call(s32[32]{0:T(128)S(1)} %and_or_fusion.targets, f32[2,32,200,128]{3,2,1,0:T(8,128)} %bitcast.6, bf16[2,32,200,128]{3,2,1,0:T(8,128)(2,1)} %bitcast.8), custom_call_target="tpu_custom_call" | custom-call | tf_op jit(solution)/shard_map/sorted/pallas_call | solution.py:111
  51.7 0.3 collective-permute-start
  52.0 2.7 %collective-permute-start.1 = (bf16[8,144,128]{2,1,0:T(8,128)(2,1)}, bf16[8,144,128]{2,1,0:T(8,128)(2,1)S(1)}, u32[]{:S(2)}, u32[]{:S(2)}) collective-permute-start(bf16[8,144,128]{2,1,0:T(8,128)(2,1)} %get-tuple-element.22), channel_id=1, source_target_pairs={{0,2},{1,3},{2,0},{3,1},{4,6},{5,7},{6,4},{7,5},{8,10},{9,11},{10,... | collective-permute-start | bytes 884744 | tf_op jit(solution)/shard_map/ppermute | solution.py:342
  54.7 0.0 collective-permute-start.2
  54.7 19.5 %collective-permute-done.refs_1_ = bf16[8,144,128]{2,1,0:T(8,128)(2,1)S(1)} collective-permute-done((bf16[8,144,128]{2,1,0:T(8,128)(2,1)}, bf16[8,144,128]{2,1,0:T(8,128)(2,1)S(1)}, u32[]{:S(2)}, u32[]{:S(2)}) %collective-permute-start) | collective-permute-done | bytes 294944 | tf_op jit(solution)/shard_map/ppermute | solution.py:342
  74.3 0.0 collective-permute-done.1.refs_2_
  74.3 8.4 %collective-permute-done.2.refs_3_ = bf16[8,144,128]{2,1,0:T(8,128)(2,1)S(1)} collective-permute-done((bf16[8,144,128]{2,1,0:T(8,128)(2,1)}, bf16[8,144,128]{2,1,0:T(8,128)(2,1)S(1)}, u32[]{:S(2)}, u32[]{:S(2)}) %collective-permute-start.2) | collective-permute-done | bytes 294944 | tf_op jit(solution)/shard_map/ppermute | solution.py:342
  82.7 1.3 %turned.1 = (bf16[4,144,128]{2,1,0:T(8,128)(2,1)S(1)}, bf16[4,144,128]{2,1,0:T(8,128)(2,1)}, bf16[4,144,128]{2,1,0:T(8,128)(2,1)}, bf16[4,144,128]{2,1,0:T(8,128...) custom-call(bf16[8,144,128]{2,1,0:T(8,128)(2,1)S(1)} %get-tuple-elem, ...), custom_call_target="tpu_custom_call" | custom-call | tf_op jit(solution)/shard_map/turned/pallas_call | solution.py:147
  83.9 0.3 collective-permute-start.3
  84.3 4.7 %collective-permute-start.4 = (bf16[4,144,128]{2,1,0:T(8,128)(2,1)}, bf16[4,144,128]{2,1,0:T(8,128)(2,1)S(1)}, u32[]{:S(2)}, u32[]{:S(2)}) collective-permute-start(bf16[4,144,128]{2,1,0:T(8,128)(2,1)} %get-tuple-element.26), channel_id=1, source_target_pairs={{0,12},{1,13},{2,14},{3,15},{4,16},{5,17},{6,18},{7,19},{8,20},{9,... | collective-permute-start | bytes 442376 | tf_op jit(solution)/shard_map/ppermute | solution.py:342
  89.0 0.4 collective-permute-start.5
  89.4 4.3 %collective-permute-start.6 = (bf16[4,144,128]{2,1,0:T(8,128)(2,1)}, bf16[4,144,128]{2,1,0:T(8,128)(2,1)S(1)}, u32[]{:S(2)}, u32[]{:S(2)}) collective-permute-start(bf16[4,144,128]{2,1,0:T(8,128)(2,1)} %get-tuple-element.28), channel_id=1, source_target_pairs={{0,20},{1,21},{2,22},{3,23},{4,24},{5,25},{6,26},{7,27},{8,28},{9,... | collective-permute-start | bytes 442376 | tf_op jit(solution)/shard_map/ppermute | solution.py:342
  93.7 3.9 %collective-permute-start.7 = (bf16[4,144,128]{2,1,0:T(8,128)(2,1)}, bf16[4,144,128]{2,1,0:T(8,128)(2,1)S(1)}, u32[]{:S(2)}, u32[]{:S(2)}) collective-permute-start(bf16[4,144,128]{2,1,0:T(8,128)(2,1)} %get-tuple-element.29), channel_id=1, source_target_pairs={{0,24},{1,25},{2,26},{3,27},{4,28},{5,29},{6,30},{7,31},{8,0},{9,1... | collective-permute-start | bytes 442376 | tf_op jit(solution)/shard_map/ppermute | solution.py:342
  97.6 7.2 %collective-permute-done.3.refs_1_.refs_2_ = bf16[4,144,128]{2,1,0:T(8,128)(2,1)S(1)} collective-permute-done((bf16[4,144,128]{2,1,0:T(8,128)(2,1)}, bf16[4,144,128]{2,1,0:T(8,128)(2,1)S(1)}, u32[]{:S(2)}, u32[]{:S(2)}) %collective-permute-start.3) | collective-permute-done | bytes 147488 | tf_op jit(solution)/shard_map/ppermute | solution.py:342
  104.8 2.8 %collective-permute-start.8 = (bf16[4,144,128]{2,1,0:T(8,128)(2,1)}, bf16[4,144,128]{2,1,0:T(8,128)(2,1)S(1)}, u32[]{:S(2)}, u32[]{:S(2)}) collective-permute-start(bf16[4,144,128]{2,1,0:T(8,128)(2,1)} %get-tuple-element.30), channel_id=1, source_target_pairs={{0,4},{1,5},{2,6},{3,7},{4,8},{5,9},{6,10},{7,11},{8,12},{9,13},{1... | collective-permute-start | bytes 442376 | tf_op jit(solution)/shard_map/ppermute | solution.py:342
  107.6 11.6 %collective-permute-done.4.refs_2_.refs_3_ = bf16[4,144,128]{2,1,0:T(8,128)(2,1)S(1)} collective-permute-done((bf16[4,144,128]{2,1,0:T(8,128)(2,1)}, bf16[4,144,128]{2,1,0:T(8,128)(2,1)S(1)}, u32[]{:S(2)}, u32[]{:S(2)}) %collective-permute-start.4) | collective-permute-done | bytes 147488 | tf_op jit(solution)/shard_map/ppermute | solution.py:342
  119.1 0.0 collective-permute-start.9
  119.2 0.7 reshape.18
  119.9 0.0 collective-permute-done.5.refs_3_.refs_4_
  119.9 0.0 collective-permute-done.6.refs_4_.refs_5_
  119.9 0.0 collective-permute-done.7.refs_5_.refs_6_
  119.9 0.1 middle.1.middle_ref
  120.0 0.0 all-to-all-done.parts_ref
  120.0 1.6 %first.1 = (bf16[2,200,4096]{2,1,0:T(8,128)(2,1)}, f32[2,128,128]{2,1,0:T(8,128)S(1)}) custom-call(bf16[32,2,128,128]{3,2,1,0:T(8,128)(2,1)S(1)} %all-to-all-done.parts_ref), custom_call_target="tpu_custom_call" | custom-call | tf_op jit(solution)/shard_map/first/pallas_call | solution.py:196
  121.5 0.0 collective-permute-done.8.refs_1_
  121.5 3.0 %collective-permute-done.9.refs_7_ = bf16[4,144,128]{2,1,0:T(8,128)(2,1)S(1)} collective-permute-done((bf16[4,144,128]{2,1,0:T(8,128)(2,1)}, bf16[4,144,128]{2,1,0:T(8,128)(2,1)S(1)}, u32[]{:S(2)}, u32[]{:S(2)}) %collective-permute-start.9) | collective-permute-done | bytes 147488 | tf_op jit(solution)/shard_map/ppermute | solution.py:342
  124.5 1.2 last.1
  (2 shorter events, 0.0 us)
Async XLA Ops:
  1.3 3.6 %collective-permute-start.10 = (bf16[2,128]{1,0:T(2,128)(2,1)S(1)}, bf16[2,128]{1,0:T(2,128)(2,1)S(1)}, u32[]{:S(2)}, u32[]{:S(2)}) collective-permute-start(bf16[2,128]{1,0:T(2,128)(2,1)S(1)} %fusion), channel_id=1, source_target_pairs={{0,1},{1,2},{2,3},{3,0},{4,5},{5,6},{6,7},{7,4},{8,9},{9,10},{10,1... | collective-permute-start | bytes 1544 | tf_op jit(solution)/shard_map/ppermute | solution.py:342
  3.5 5.1 %collective-permute-start.11 = (bf16[2,128]{1,0:T(2,128)(2,1)S(1)}, bf16[2,128]{1,0:T(2,128)(2,1)S(1)}, u32[]{:S(2)}, u32[]{:S(2)}) collective-permute-start(bf16[2,128]{1,0:T(2,128)(2,1)S(1)} %fusion), channel_id=1, source_target_pairs={{0,2},{1,3},{2,0},{3,1},{4,6},{5,7},{6,4},{7,5},{8,10},{9,11},{10,... | collective-permute-start | bytes 1544 | tf_op jit(solution)/shard_map/ppermute | solution.py:342
  4.2 4.8 %collective-permute-start.12 = (bf16[2,128]{1,0:T(2,128)(2,1)S(1)}, bf16[2,128]{1,0:T(2,128)(2,1)S(1)}, u32[]{:S(2)}, u32[]{:S(2)}) collective-permute-start(bf16[2,128]{1,0:T(2,128)(2,1)S(1)} %fusion), channel_id=1, source_target_pairs={{0,3},{1,0},{2,1},{3,2},{4,7},{5,4},{6,5},{7,6},{8,11},{9,8},{10,9... | collective-permute-start | bytes 1544 | tf_op jit(solution)/shard_map/ppermute | solution.py:342
  9.0 14.8 %collective-permute-start.13 = (bf16[8,128]{1,0:T(8,128)(2,1)S(1)}, bf16[8,128]{1,0:T(8,128)(2,1)S(1)}, u32[]{:S(2)}, u32[]{:S(2)}) collective-permute-start(bf16[8,128]{1,0:T(8,128)(2,1)S(1)} %pad_maximum_fusion.refs_0_), channel_id=1, source_target_pairs={{0,4},{1,5},{2,6},{3,7},{4,8},{5,9},{6,10},{7,11},{8,12},{9,13},{1... | collective-permute-start | bytes 6152 | tf_op jit(solution)/shard_map/ppermute | solution.py:342
  11.0 15.5 %collective-permute-start.14 = (bf16[8,128]{1,0:T(8,128)(2,1)S(1)}, bf16[8,128]{1,0:T(8,128)(2,1)S(1)}, u32[]{:S(2)}, u32[]{:S(2)}) collective-permute-start(bf16[8,128]{1,0:T(8,128)(2,1)S(1)} %pad_maximum_fusion.refs_0_), channel_id=1, source_target_pairs={{0,8},{1,9},{2,10},{3,11},{4,12},{5,13},{6,14},{7,15},{8,16},{9,17... | collective-permute-start | bytes 6152 | tf_op jit(solution)/shard_map/ppermute | solution.py:342
  14.3 13.2 %collective-permute-start.15 = (bf16[8,128]{1,0:T(8,128)(2,1)S(1)}, bf16[8,128]{1,0:T(8,128)(2,1)S(1)}, u32[]{:S(2)}, u32[]{:S(2)}) collective-permute-start(bf16[8,128]{1,0:T(8,128)(2,1)S(1)} %pad_maximum_fusion.refs_0_), channel_id=1, source_target_pairs={{0,12},{1,13},{2,14},{3,15},{4,16},{5,17},{6,18},{7,19},{8,20},{9,... | collective-permute-start | bytes 6152 | tf_op jit(solution)/shard_map/ppermute | solution.py:342
  18.3 9.2 %collective-permute-start.16 = (bf16[8,128]{1,0:T(8,128)(2,1)S(1)}, bf16[8,128]{1,0:T(8,128)(2,1)S(1)}, u32[]{:S(2)}, u32[]{:S(2)}) collective-permute-start(bf16[8,128]{1,0:T(8,128)(2,1)S(1)} %pad_maximum_fusion.refs_0_), channel_id=1, source_target_pairs={{0,16},{1,17},{2,18},{3,19},{4,20},{5,21},{6,22},{7,23},{8,24},{9,... | collective-permute-start | bytes 6152 | tf_op jit(solution)/shard_map/ppermute | solution.py:342
  18.9 8.6 %collective-permute-start.17 = (bf16[8,128]{1,0:T(8,128)(2,1)S(1)}, bf16[8,128]{1,0:T(8,128)(2,1)S(1)}, u32[]{:S(2)}, u32[]{:S(2)}) collective-permute-start(bf16[8,128]{1,0:T(8,128)(2,1)S(1)} %pad_maximum_fusion.refs_0_), channel_id=1, source_target_pairs={{0,20},{1,21},{2,22},{3,23},{4,24},{5,25},{6,26},{7,27},{8,28},{9,... | collective-permute-start | bytes 6152 | tf_op jit(solution)/shard_map/ppermute | solution.py:342
  23.8 4.5 %collective-permute-start.18 = (bf16[8,128]{1,0:T(8,128)(2,1)S(1)}, bf16[8,128]{1,0:T(8,128)(2,1)S(1)}, u32[]{:S(2)}, u32[]{:S(2)}) collective-permute-start(bf16[8,128]{1,0:T(8,128)(2,1)S(1)} %pad_maximum_fusion.refs_0_), channel_id=1, source_target_pairs={{0,24},{1,25},{2,26},{3,27},{4,28},{5,29},{6,30},{7,31},{8,0},{9,1... | collective-permute-start | bytes 6152 | tf_op jit(solution)/shard_map/ppermute | solution.py:342
  26.5 3.6 %collective-permute-start.19 = (bf16[8,128]{1,0:T(8,128)(2,1)S(1)}, bf16[8,128]{1,0:T(8,128)(2,1)S(1)}, u32[]{:S(2)}, u32[]{:S(2)}) collective-permute-start(bf16[8,128]{1,0:T(8,128)(2,1)S(1)} %pad_maximum_fusion.refs_0_), channel_id=1, source_target_pairs={{0,28},{1,29},{2,30},{3,31},{4,0},{5,1},{6,2},{7,3},{8,4},{9,5},{1... | collective-permute-start | bytes 6152 | tf_op jit(solution)/shard_map/ppermute | solution.py:342
  30.8 10.6 %all-to-all-start.1 = ((bf16[8,2,4096]{2,1,0:T(2,128)(2,1)}), bf16[8,2,4096]{2,1,0:T(2,128)(2,1)S(1)}, u32[]{:S(2)}, u32[]{:S(2)}) async-start(bf16[8,2,4096]{2,1,0:T(2,128)(2,1)} %router.1), calls=%async_computation.1 | async-start | bytes 262144 | tf_op jit(solution)/shard_map/all_to_all | solution.py:372
  41.4 78.5 %all-to-all-start = ((bf16[32,2,128,128]{3,2,1,0:T(8,128)(2,1)}), bf16[32,2,128,128]{3,2,1,0:T(8,128)(2,1)S(1)}, u32[]{:S(2)}, u32[]{:S(2)}) async-start(bf16[32,2,128,128]{3,2,1,0:T(8,128)(2,1)} %packed.1), calls=%async_computation | async-start | bytes 4194304 | tf_op jit(solution)/shard_map/all_to_all | solution.py:357
  51.7 22.5 %collective-permute-start = (bf16[8,144,128]{2,1,0:T(8,128)(2,1)}, bf16[8,144,128]{2,1,0:T(8,128)(2,1)S(1)}, u32[]{:S(2)}, u32[]{:S(2)}) collective-permute-start(bf16[8,144,128]{2,1,0:T(8,128)(2,1)} %get-tuple-element.21), channel_id=1, source_target_pairs={{0,1},{1,2},{2,3},{3,0},{4,5},{5,6},{6,7},{7,4},{8,9},{9,10},{10,1... | collective-permute-start | bytes 884744 | tf_op jit(solution)/shard_map/ppermute | solution.py:342
  52.0 22.2 %collective-permute-start.1 = (bf16[8,144,128]{2,1,0:T(8,128)(2,1)}, bf16[8,144,128]{2,1,0:T(8,128)(2,1)S(1)}, u32[]{:S(2)}, u32[]{:S(2)}) collective-permute-start(bf16[8,144,128]{2,1,0:T(8,128)(2,1)} %get-tuple-element.22), channel_id=1, source_target_pairs={{0,2},{1,3},{2,0},{3,1},{4,6},{5,7},{6,4},{7,5},{8,10},{9,11},{10,... | collective-permute-start | bytes 884744 | tf_op jit(solution)/shard_map/ppermute | solution.py:342
  54.7 27.9 %collective-permute-start.2 = (bf16[8,144,128]{2,1,0:T(8,128)(2,1)}, bf16[8,144,128]{2,1,0:T(8,128)(2,1)S(1)}, u32[]{:S(2)}, u32[]{:S(2)}) collective-permute-start(bf16[8,144,128]{2,1,0:T(8,128)(2,1)} %get-tuple-element.23), channel_id=1, source_target_pairs={{0,3},{1,0},{2,1},{3,2},{4,7},{5,4},{6,5},{7,6},{8,11},{9,8},{10,9... | collective-permute-start | bytes 884744 | tf_op jit(solution)/shard_map/ppermute | solution.py:342
  83.9 20.8 %collective-permute-start.3 = (bf16[4,144,128]{2,1,0:T(8,128)(2,1)}, bf16[4,144,128]{2,1,0:T(8,128)(2,1)S(1)}, u32[]{:S(2)}, u32[]{:S(2)}) collective-permute-start(bf16[4,144,128]{2,1,0:T(8,128)(2,1)} %get-tuple-element.25), channel_id=1, source_target_pairs={{0,8},{1,9},{2,10},{3,11},{4,12},{5,13},{6,14},{7,15},{8,16},{9,17... | collective-permute-start | bytes 442376 | tf_op jit(solution)/shard_map/ppermute | solution.py:342
  84.3 34.9 %collective-permute-start.4 = (bf16[4,144,128]{2,1,0:T(8,128)(2,1)}, bf16[4,144,128]{2,1,0:T(8,128)(2,1)S(1)}, u32[]{:S(2)}, u32[]{:S(2)}) collective-permute-start(bf16[4,144,128]{2,1,0:T(8,128)(2,1)} %get-tuple-element.26), channel_id=1, source_target_pairs={{0,12},{1,13},{2,14},{3,15},{4,16},{5,17},{6,18},{7,19},{8,20},{9,... | collective-permute-start | bytes 442376 | tf_op jit(solution)/shard_map/ppermute | solution.py:342
  89.0 30.9 %collective-permute-start.5 = (bf16[4,144,128]{2,1,0:T(8,128)(2,1)}, bf16[4,144,128]{2,1,0:T(8,128)(2,1)S(1)}, u32[]{:S(2)}, u32[]{:S(2)}) collective-permute-start(bf16[4,144,128]{2,1,0:T(8,128)(2,1)} %get-tuple-element.27), channel_id=1, source_target_pairs={{0,16},{1,17},{2,18},{3,19},{4,20},{5,21},{6,22},{7,23},{8,24},{9,... | collective-permute-start | bytes 442376 | tf_op jit(solution)/shard_map/ppermute | solution.py:342
  89.4 30.4 %collective-permute-start.6 = (bf16[4,144,128]{2,1,0:T(8,128)(2,1)}, bf16[4,144,128]{2,1,0:T(8,128)(2,1)S(1)}, u32[]{:S(2)}, u32[]{:S(2)}) collective-permute-start(bf16[4,144,128]{2,1,0:T(8,128)(2,1)} %get-tuple-element.28), channel_id=1, source_target_pairs={{0,20},{1,21},{2,22},{3,23},{4,24},{5,25},{6,26},{7,27},{8,28},{9,... | collective-permute-start | bytes 442376 | tf_op jit(solution)/shard_map/ppermute | solution.py:342
  93.7 26.2 %collective-permute-start.7 = (bf16[4,144,128]{2,1,0:T(8,128)(2,1)}, bf16[4,144,128]{2,1,0:T(8,128)(2,1)S(1)}, u32[]{:S(2)}, u32[]{:S(2)}) collective-permute-start(bf16[4,144,128]{2,1,0:T(8,128)(2,1)} %get-tuple-element.29), channel_id=1, source_target_pairs={{0,24},{1,25},{2,26},{3,27},{4,28},{5,29},{6,30},{7,31},{8,0},{9,1... | collective-permute-start | bytes 442376 | tf_op jit(solution)/shard_map/ppermute | solution.py:342
  104.8 16.7 %collective-permute-start.8 = (bf16[4,144,128]{2,1,0:T(8,128)(2,1)}, bf16[4,144,128]{2,1,0:T(8,128)(2,1)S(1)}, u32[]{:S(2)}, u32[]{:S(2)}) collective-permute-start(bf16[4,144,128]{2,1,0:T(8,128)(2,1)} %get-tuple-element.30), channel_id=1, source_target_pairs={{0,4},{1,5},{2,6},{3,7},{4,8},{5,9},{6,10},{7,11},{8,12},{9,13},{1... | collective-permute-start | bytes 442376 | tf_op jit(solution)/shard_map/ppermute | solution.py:342
  119.1 5.4 %collective-permute-start.9 = (bf16[4,144,128]{2,1,0:T(8,128)(2,1)}, bf16[4,144,128]{2,1,0:T(8,128)(2,1)S(1)}, u32[]{:S(2)}, u32[]{:S(2)}) collective-permute-start(bf16[4,144,128]{2,1,0:T(8,128)(2,1)} %get-tuple-element.31), channel_id=1, source_target_pairs={{0,28},{1,29},{2,30},{3,31},{4,0},{5,1},{6,2},{7,3},{8,4},{9,5},{1... | collective-permute-start | bytes 442376 | tf_op jit(solution)/shard_map/ppermute | solution.py:342
